TPU v7x, 32 devices: a whole 2x2x4 slice. The times are simulated.
32 devices in a mesh: dp: 8 (over z, x), tensor: 4 (over y, core).
Axes of the slice: x: 2, y: 2, z: 4, core: 2. Of those that a mesh axis runs over, the one named last changes fastest.
Arguments:
- tokens: bfloat16 [20480, 768], P(('dp', 'tensor')), may hold values from -6 to 6
- cotangent: bfloat16 [20480, 768], P(('dp', 'tensor')), may hold values from -6 to 6
- lengths: int32 [8, 8], P('dp'), may hold values from 1 to 512, 2048 in all within a row
- w_qkv: bfloat16 [768, 3, 768], P('dp', None, 'tensor'), may hold values from -0.21875 to 0.21875
- w_out: bfloat16 [768, 768], P('tensor', 'dp'), may hold values from -6 to 6
- w_fc: bfloat16 [768, 3072], P('dp', 'tensor'), may hold values from -0.21875 to 0.21875
- w_proj: bfloat16 [3072, 768], P('tensor', 'dp'), may hold values from -0.109375 to 0.109375
- ln1_gain: bfloat16 [768], P('dp'), may hold values from 0.25 to 1.75
- ln1_bias: bfloat16 [768], P('dp'), may hold values from -3 to 3
- ln2_gain: bfloat16 [768], P('dp'), may hold values from 0.25 to 1.75
- ln2_bias: bfloat16 [768], P('dp'), may hold values from -3 to 3
Outputs:
- block_out: bfloat16 [20480, 768], P(('dp', 'tensor'))
- input_grad: bfloat16 [20480, 768], P(('dp', 'tensor'))
- w_qkv_grad: float32 [768, 3, 768], P('dp', None, 'tensor')
- w_out_grad: float32 [768, 768], P('tensor', 'dp')
- w_fc_grad: float32 [768, 3072], P('dp', 'tensor')
- w_proj_grad: float32 [3072, 768], P('tensor', 'dp')
- ln1_gain_grad: float32 [768], P('dp')
- ln1_bias_grad: float32 [768], P('dp')
- ln2_gain_grad: float32 [768], P('dp')
- ln2_bias_grad: float32 [768], P('dp')
Inputs may be any that keep to these rules, and one draw needn't show every extreme that they name: `lengths`: row g lists the token counts of group g's 8 continuations in order after its 512-token prompt; each row sums to 2048 and its largest entry is exactly 512.
All inputs are finite; a program needn't handle non-finite values.
Results may differ from a plain program's by a relative error of at most 0.019.
The roundings to bfloat16 on the way count: a program that leaves them out, or rounds other values in their place, can miss the bound.
Values may be sent and summed in bfloat16 or wider, within the bound.
A program may use at most 192 MiB of HBM per device.

v0:
```python
import jax
import jax.numpy as jnp
from jax import lax
from jax.sharding import PartitionSpec as P

HEAD = 64
PROMPT = 512


def normalize(values):
    mean = jnp.mean(values, axis=-1, keepdims=True)
    centred = values - mean
    spread = jnp.mean(centred * centred, axis=-1, keepdims=True)
    factor = lax.rsqrt(spread + 1e-05)
    return (centred * factor, factor)


def norm_back(grad_out, normed, factor, gain):
    scaled = grad_out * gain
    first = jnp.mean(scaled, axis=-1, keepdims=True)
    second = jnp.mean(scaled * normed, axis=-1, keepdims=True)
    return factor * (scaled - first - normed * second)


def gelu_tanh(values):
    return jax.nn.gelu(values, approximate=True)


def inner_rows(left, right):
    return lax.dot_general(
        left, right, (((0,), (0,)), ((), ())), preferred_element_type=jnp.float32
    )


def times_trans(left, right):
    return lax.dot_general(
        left, right, (((1,), (1,)), ((), ())), preferred_element_type=jnp.float32
    )


def segment_ids(lengths, total):
    ends = PROMPT + jnp.cumsum(lengths[0])
    places = jnp.arange(total, dtype=jnp.int32)
    passed = jnp.sum((places[:, None] >= ends[None, :]).astype(jnp.int32), axis=1)
    return (places, jnp.where(places < PROMPT, -1, passed))


def visible(query_pos, query_seg, key_pos, key_seg):
    causal = key_pos[None, :] <= query_pos[:, None]
    shared = (key_seg[None, :] < 0) | (key_seg[None, :] == query_seg[:, None])
    return (causal & shared)[None]


def attend(queries, keys, values, places, segs, block, scale):
    count = queries.shape[0] // block

    def one(index):
        start = index * block
        query = lax.dynamic_slice_in_dim(queries, start, block, 0)
        mask = visible(
            lax.dynamic_slice_in_dim(places, start, block, 0),
            lax.dynamic_slice_in_dim(segs, start, block, 0),
            places,
            segs,
        )
        raw = jnp.einsum("qhd,khd->hqk", query, keys, preferred_element_type=jnp.float32) * scale
        magnitude = jnp.where(mask, jnp.abs(raw), -1e30)
        top = jnp.max(magnitude, axis=-1, keepdims=True)
        expo = jnp.where(mask, jnp.exp(magnitude - top), 0.0)
        total = jnp.sum(expo, axis=-1, keepdims=True)
        weights = (jnp.sign(raw) * (expo / total)).astype(jnp.bfloat16)
        mixed = jnp.einsum("hqk,khd->qhd", weights, values, preferred_element_type=jnp.float32)
        return (mixed.astype(jnp.bfloat16), (top + jnp.log(total))[..., 0])

    mixed, sums = lax.map(one, jnp.arange(count, dtype=jnp.int32))
    return (mixed.reshape(queries.shape[0], -1), sums)


def attend_back(queries, keys, values, grad_mixed, sums, places, segs, block, scale):
    count = queries.shape[0] // block

    def step(carry, inputs):
        key_grad, value_grad = carry
        index, lse_block = inputs
        start = index * block
        query = lax.dynamic_slice_in_dim(queries, start, block, 0)
        grad_block = lax.dynamic_slice_in_dim(grad_mixed, start, block, 0)
        mask = visible(
            lax.dynamic_slice_in_dim(places, start, block, 0),
            lax.dynamic_slice_in_dim(segs, start, block, 0),
            places,
            segs,
        )
        raw = jnp.einsum("qhd,khd->hqk", query, keys, preferred_element_type=jnp.float32) * scale
        prob = jnp.where(mask, jnp.exp(jnp.abs(raw) - lse_block[..., None]), 0.0)
        signed = jnp.sign(raw) * prob
        rounded = signed.astype(jnp.bfloat16)
        value_grad = value_grad + jnp.einsum(
            "hqk,qhd->khd", rounded, grad_block, preferred_element_type=jnp.float32
        )
        weight_grad = jnp.einsum(
            "qhd,khd->hqk", grad_block, values, preferred_element_type=jnp.float32
        )
        inner = jnp.sum(signed * weight_grad, axis=-1, keepdims=True)
        score_grad = (prob * weight_grad - signed * inner).astype(jnp.bfloat16)
        query_grad = (
            jnp.einsum("hqk,khd->qhd", score_grad, keys, preferred_element_type=jnp.float32) * scale
        )
        key_grad = (
            key_grad
            + jnp.einsum("hqk,qhd->khd", score_grad, query, preferred_element_type=jnp.float32)
            * scale
        )
        return ((key_grad, value_grad), query_grad)

    zeros = jnp.zeros(keys.shape, jnp.float32)
    (key_grad, value_grad), query_grad = lax.scan(
        step, (zeros, zeros), (jnp.arange(count, dtype=jnp.int32), sums)
    )
    return (query_grad.reshape(keys.shape), key_grad, value_grad)


def on_device(
    tokens, cotangent, lengths, w_qkv, w_out, w_fc, w_proj, ln1_gain, ln1_bias, ln2_gain, ln2_bias
):
    rows = tokens.shape[0]
    group = rows * lax.axis_size("tensor")
    block = group // max(1, group // 512)
    scale = HEAD ** (-0.5)
    pieces = (w_qkv, w_out, w_fc, w_proj, ln1_gain, ln1_bias, ln2_gain, ln2_bias)
    qkv_full, out_full, fc_full, proj_full, gain1, bias1, gain2, bias2 = (
        lax.all_gather(pieces[0], "dp", axis=0, tiled=True),
        lax.all_gather(pieces[1], "dp", axis=1, tiled=True),
        lax.all_gather(pieces[2], "dp", axis=0, tiled=True),
        lax.all_gather(pieces[3], "dp", axis=1, tiled=True),
        lax.all_gather(pieces[4], "dp", axis=0, tiled=True),
        lax.all_gather(pieces[5], "dp", axis=0, tiled=True),
        lax.all_gather(pieces[6], "dp", axis=0, tiled=True),
        lax.all_gather(pieces[7], "dp", axis=0, tiled=True),
    )
    gain1 = gain1.astype(jnp.float32)
    bias1 = bias1.astype(jnp.float32)
    gain2 = gain2.astype(jnp.float32)
    bias2 = bias2.astype(jnp.float32)
    width = qkv_full.shape[0]
    local = qkv_full.shape[2]
    heads = local // HEAD
    qkv_mat = qkv_full.reshape(width, 3 * local)
    places, segs = segment_ids(lengths, group)
    inputs = tokens.astype(jnp.float32)
    normed1, factor1 = normalize(inputs)
    lowered1 = (normed1 * gain1 + bias1).astype(jnp.bfloat16)
    all_norm1 = lax.all_gather(lowered1, "tensor", axis=0, tiled=True)
    projected = jnp.dot(all_norm1, qkv_mat, preferred_element_type=jnp.float32).astype(jnp.bfloat16)
    projected = projected.reshape(group, 3, heads, HEAD)
    queries = projected[:, 0]
    keys = projected[:, 1]
    values = projected[:, 2]
    mixed, sums = attend(queries, keys, values, places, segs, block, scale)
    part = mixed
    resid = inputs + lax.psum_scatter(
        jnp.dot(part, out_full, preferred_element_type=jnp.float32).astype(jnp.bfloat16),
        "tensor",
        scatter_dimension=0,
        tiled=True,
    ).astype(jnp.float32)
    normed2, factor2 = normalize(resid)
    lowered2 = (normed2 * gain2 + bias2).astype(jnp.bfloat16)
    all_norm2 = lax.all_gather(lowered2, "tensor", axis=0, tiled=True)
    hidden_pre = jnp.dot(all_norm2, fc_full, preferred_element_type=jnp.float32)
    hidden, gelu_pull = jax.vjp(gelu_tanh, hidden_pre)
    hidden_low = hidden.astype(jnp.bfloat16)
    part = hidden_low
    mlp_rows = lax.psum_scatter(
        jnp.dot(part, proj_full, preferred_element_type=jnp.float32).astype(jnp.bfloat16),
        "tensor",
        scatter_dimension=0,
        tiled=True,
    ).astype(jnp.float32)
    block_out = (resid + mlp_rows).astype(jnp.bfloat16)
    grad_all = lax.all_gather(cotangent, "tensor", axis=0, tiled=True)
    hidden_grad = times_trans(grad_all, proj_full)
    proj_grad = inner_rows(hidden_low, grad_all)
    pre_low = gelu_pull(hidden_grad)[0].astype(jnp.bfloat16)
    fc_grad = inner_rows(all_norm2, pre_low)
    part = pre_low
    norm2_grad = lax.psum_scatter(
        times_trans(part, fc_full).astype(jnp.bfloat16), "tensor", scatter_dimension=0, tiled=True
    ).astype(jnp.float32)
    gain2_part = jnp.sum(norm2_grad * normed2, axis=0)
    bias2_part = jnp.sum(norm2_grad, axis=0)
    resid_grad = cotangent.astype(jnp.float32) + norm_back(norm2_grad, normed2, factor2, gain2)
    resid_low = resid_grad.astype(jnp.bfloat16)
    resid_all = lax.all_gather(resid_low, "tensor", axis=0, tiled=True)
    out_grad = inner_rows(mixed, resid_all)
    mixed_grad = times_trans(resid_all, out_full).astype(jnp.bfloat16).reshape(group, heads, HEAD)
    query_grad, key_grad, value_grad = attend_back(
        queries, keys, values, mixed_grad, sums, places, segs, block, scale
    )
    qkv_grad_low = (
        jnp.stack([query_grad, key_grad, value_grad], axis=1)
        .astype(jnp.bfloat16)
        .reshape(group, 3 * local)
    )
    qkv_grad = inner_rows(all_norm1, qkv_grad_low).reshape(width, 3, local)
    part = qkv_grad_low
    norm1_grad = lax.psum_scatter(
        times_trans(part, qkv_mat).astype(jnp.bfloat16), "tensor", scatter_dimension=0, tiled=True
    ).astype(jnp.float32)
    gain1_part = jnp.sum(norm1_grad * normed1, axis=0)
    bias1_part = jnp.sum(norm1_grad, axis=0)
    input_grad = (resid_grad + norm_back(norm1_grad, normed1, factor1, gain1)).astype(jnp.bfloat16)
    qkv_sum, out_sum, fc_sum, proj_sum, gain1_share, bias1_share, gain2_share, bias2_share = (
        lax.psum_scatter(qkv_grad, "dp", scatter_dimension=0, tiled=True),
        lax.psum_scatter(out_grad, "dp", scatter_dimension=1, tiled=True),
        lax.psum_scatter(fc_grad, "dp", scatter_dimension=0, tiled=True),
        lax.psum_scatter(proj_grad, "dp", scatter_dimension=1, tiled=True),
        lax.psum_scatter(gain1_part, "dp", scatter_dimension=0, tiled=True),
        lax.psum_scatter(bias1_part, "dp", scatter_dimension=0, tiled=True),
        lax.psum_scatter(gain2_part, "dp", scatter_dimension=0, tiled=True),
        lax.psum_scatter(bias2_part, "dp", scatter_dimension=0, tiled=True),
    )
    gain1_sum, bias1_sum, gain2_sum, bias2_sum = lax.psum(
        (gain1_share, bias1_share, gain2_share, bias2_share), "tensor"
    )
    return (
        block_out,
        input_grad,
        qkv_sum,
        out_sum,
        fc_sum,
        proj_sum,
        gain1_sum,
        bias1_sum,
        gain2_sum,
        bias2_sum,
    )


def solution(mesh):
    placed = (
        P(("dp", "tensor"), None),
        P(("dp", "tensor"), None),
        P("dp", None),
        P("dp", None, "tensor"),
        P("tensor", "dp"),
        P("dp", "tensor"),
        P("tensor", "dp"),
        P("dp"),
        P("dp"),
        P("dp"),
        P("dp"),
    )
    return jax.shard_map(
        on_device,
        mesh=mesh,
        in_specs=placed,
        out_specs=(
            P(("dp", "tensor"), None),
            P(("dp", "tensor"), None),
            P("dp", None, "tensor"),
            P("tensor", "dp"),
            P("dp", "tensor"),
            P("tensor", "dp"),
            P("dp"),
            P("dp"),
            P("dp"),
            P("dp"),
        ),
        check_vma=False,
    )
```

profile of v0, /device:TPU:0, one launch (start us, length us, event | category | flops | bytes accessed | tf_op | source)
XLA Modules:
  0.0 1164.4 jit_solution(4583404668944278764)
XLA Ops:
  13.4 23.9 %all-reduce.10 = (bf16[768]{0:T(1024)(128)(2,1)}, bf16[768]{0:T(1024)(128)(2,1)}, bf16[768]{0:T(1024)(128)(2,1)S(1)}, bf16[768]{0:T(1024)(128)(2,1)S(1)}) all-reduce(bf16[768]{0:T(1024)(128)(2,1)S(1)} %dynamic-update-slice.3, bf16[768]{0:T(1024)(128)(2,1)S(1)} %dynamic-update-slice.2, ...), channel_id=1, replica_groups=mesh['dp'=8,'tensor'=4] {'dp'}, use_global_device_ids=true, to_apply=%add.3 | all-reduce | flops 3072 | bytes 12288
  43.6 35.5 %all_gather.39 = bf16[768,3,192]{2,1,0:T(4,128)(2,1)S(1)} all-gather(bf16[96,3,192]{2,1,0:T(4,128)(2,1)S(1)} %copy.32), channel_id=1, replica_groups=mesh['dp'=8,'tensor'=4] {'dp'}, dimensions={0}, use_global_device_ids=true | all-gather | bytes 995328 | tf_op jit(solution)/shard_map/all_gather | solution.py:132
  80.1 33.6 %all_gather.40 = bf16[192,768]{0,1:T(8,128)(2,1)} all-gather(bf16[192,96]{0,1:T(8,128)(2,1)S(1)} %copy.35), channel_id=1, replica_groups=mesh['dp'=8,'tensor'=4] {'dp'}, dimensions={1}, use_global_device_ids=true | all-gather | bytes 331776 | tf_op jit(solution)/shard_map/all_gather | solution.py:133
  113.7 4.6 convolution_convert_fusion.4
  119.7 122.1 %while.29 = (s32[]{:T(128)}, bf16[5,512,3,64]{1,3,2,0:T(8,128)(2,1)S(1)}, f32[5,3,512]{2,1,0:T(4,128)S(1)}, s32[5]{0:T(128)S(1)}, bf16[2560,3,64]{0,2,1:T(8,128)...) while((s32[]{:T(128)}, ...), condition=%wide.region_7.8_spmd.clone, body=%wide.region_4.7_spmd.clone.sunk | while | flops 1086686208 | bytes 54895824 | solution.py:75
  122.9 5.1 fusion.125
  128.0 5.5 fusion.126
  133.5 10.6 fusion.127
  147.3 5.1 fusion.125
  152.4 5.5 fusion.126
  157.8 10.6 fusion.127
  171.7 5.1 fusion.125
  176.8 5.5 fusion.126
  182.2 10.6 fusion.127
  196.1 5.1 fusion.125
  201.2 5.5 fusion.126
  206.6 10.6 fusion.127
  220.4 5.1 fusion.125
  225.5 5.5 fusion.126
  231.0 10.6 fusion.127
  248.8 40.7 %reduce-scatter.11.cloned.1.call-done = bf16[640,768]{1,0:T(8,128)(2,1)} async-done(((bf16[2560,768]{1,0:T(8,128)(2,1)}), bf16[640,768]{1,0:T(8,128)(2,1)}) %reduce-scatter.11.cloned.1.call-update) | async-done | bytes 983056 | tf_op jit(solution)/shard_map/reduce_scatter | solution.py:161
  294.4 28.8 %all-gather.15.cloned.1.call-done = bf16[2560,768]{1,0:T(8,128)(2,1)} async-done(((bf16[640,768]{1,0:T(8,128)(2,1)}), bf16[2560,768]{1,0:T(8,128)(2,1)}) %all-gather.15.cloned.1.call-update) | async-done | bytes 3932176 | tf_op jit(solution)/shard_map/all_gather | solution.py:181
  323.2 8.8 fusion.75
  332.1 34.7 %all-gather.11.cloned.1.call-done = bf16[768,768]{1,0:T(8,128)(2,1)} async-done(((bf16[96,768]{1,0:T(8,128)(2,1)}), bf16[768,768]{1,0:T(8,128)(2,1)}) %all-gather.11.cloned.1.call-update) | async-done | bytes 1179664 | tf_op jit(solution)/shard_map/all_gather | solution.py:134
  366.7 33.4 %all-gather.9.cloned.1.call-done = bf16[2560,768]{1,0:T(8,128)(2,1)} async-done(((bf16[640,768]{1,0:T(8,128)(2,1)}), bf16[2560,768]{1,0:T(8,128)(2,1)}) %all-gather.9.cloned.1.call-update) | async-done | bytes 3932176 | tf_op jit(solution)/shard_map/all_gather | solution.py:169
  400.1 13.6 %fusion.43 = (bf16[2560,768]{1,0:T(8,128)(2,1)S(1)}, f32[2560,768]{1,0:T(8,128)}) fusion(f32[2560,768]{1,0:T(8,128)} %fusion.75, bf16[2560,768]{1,0:T(8,128)(2,1)} %all-gather.9.cloned.1.call-done, bf16[768,768]{1,0:T(8,128)(2,1)} %all-gather.11.cloned.1.call-done), kind=kOutput, calls=%fused_computation.55 | convolution fusion | flops 3059220480 | bytes 24772608 | tf_op jit(solution)/shard_map/dot_general | solution.py:170
  415.7 4.8 convolution_convert_fusion
  421.0 42.6 %reduce-scatter.15.cloned.1.call-done = bf16[640,768]{1,0:T(8,128)(2,1)} async-done(((bf16[2560,768]{1,0:T(8,128)(2,1)}), bf16[640,768]{1,0:T(8,128)(2,1)}) %reduce-scatter.15.cloned.1.call-update) | async-done | bytes 983056 | tf_op jit(solution)/shard_map/reduce_scatter | solution.py:187
  467.0 3.4 fusion.72
  470.5 32.9 %all-gather.17.cloned.1.call-done = bf16[2560,768]{1,0:T(8,128)(2,1)} async-done(((bf16[640,768]{1,0:T(8,128)(2,1)}), bf16[2560,768]{1,0:T(8,128)(2,1)}) %all-gather.17.cloned.1.call-update) | async-done | bytes 3932176 | tf_op jit(solution)/shard_map/all_gather | solution.py:194
  503.4 4.9 convolution_bitcast_fusion
  508.4 4.5 convolution_convert_fusion.5
  512.9 323.7 %while.30 = (s32[]{:T(128)}, f32[2560,3,64]{0,2,1:T(8,128)}, f32[2560,3,64]{0,2,1:T(8,128)}, bf16[5,512,3,64]{1,0,3,2:T(8,128)(2,1)}, s32[5]{0:T(128)S(1)}, /*in...) while((s32[]{:T(128)}, f32[2560,3,64]{0,2,1:T(8,128)}, ...), condition=%wide.region_17.18_spmd.clone.clone, body=%wide.region_15.17_spmd.clone.clone.sunk | while | flops 2622784512 | bytes 218457456 | solution.py:117
  519.5 12.2 %fusion.139 = f32[2560,3,64]{0,2,1:T(8,128)} fusion(f32[3,512,2560]{2,1,0:T(8,128)S(1)} %fusion.137, f32[3,512]{1,0:T(4,128)S(1)} %dynamic-slice_bitcast_fusion.2, pred[512,2560]{1,0:T(8,128)(4,1)S(1)} %or_and_fusion.5, f32[2560,3,64]{0,2,1:T(8,128)} %get-tuple-element.492, pred[]{:T(512)S(6)} %compare.3, ...), kind=kOutput, calls=%fused_computation.30.clone.1 | convolution fusion | flops 531824640 | bytes 21174276 | tf_op jit(solution)/shard_map/while/body/eval_jaxpr/hqk,qhd->khd/dot_general | solution.py:98
  531.7 15.0 %multiply_reduce_fusion.3 = (f32[3,512]{1,0:T(4,128)S(1)}, f32[3,512,2560]{2,1,0:T(8,128)}) fusion(f32[3,512,2560]{2,1,0:T(8,128)S(1)} %fusion.137, f32[3,512]{1,0:T(4,128)S(1)} %dynamic-slice_bitcast_fusion.2, pred[512,2560]{1,0:T(8,128)(4,1)S(1)} %or_and_fusion.5, bf16[2560,3,64]{0,2,1:T(8,128)(2,1)S(1)} %copy-done.12, ...), kind=kOutput, calls=%fused_computation.19.clone.1 | convolution fusion | flops 534772224 | bytes 33959940 | tf_op jit(solution)/shard_map/while/body/eval_jaxpr/qhd,khd->hqk/dot_general | solution.py:101
  546.7 15.2 %subtract_convert_fusion.2 = bf16[3,512,2560]{2,1,0:T(8,128)(2,1)S(1)} fusion(f32[3,512,2560]{2,1,0:T(8,128)} %get-tuple-element.433, f32[3,512,2560]{2,1,0:T(8,128)} %copy-done, f32[3,512]{1,0:T(4,128)S(1)} %get-tuple-element.434, f32[3,512]{1,0:T(4,128)S(1)} %dynamic-slice_bitcast_fusion.2, pred[512,2560]{1,0:T(8,128)(4,1)S(1)} %or_and_fusion.5), kind=kLoop, calls=%fused_computation.18.clone.1 | loop fusion | flops 39321600 | bytes 40644608 | tf_op jit(solution)/shard_map/while/body/eval_jaxpr/convert_element_type | solution.py:105
  567.3 8.7 dynamic_update_slice.23
  582.4 14.4 %fusion.139 = f32[2560,3,64]{0,2,1:T(8,128)} fusion(f32[3,512,2560]{2,1,0:T(8,128)S(1)} %fusion.137, f32[3,512]{1,0:T(4,128)S(1)} %dynamic-slice_bitcast_fusion.2, pred[512,2560]{1,0:T(8,128)(4,1)S(1)} %or_and_fusion.5, f32[2560,3,64]{0,2,1:T(8,128)} %get-tuple-element.492, pred[]{:T(512)S(6)} %compare.3, ...), kind=kOutput, calls=%fused_computation.30.clone.1 | convolution fusion | flops 531824640 | bytes 21174276 | tf_op jit(solution)/shard_map/while/body/eval_jaxpr/hqk,qhd->khd/dot_general | solution.py:98
  596.8 15.0 %multiply_reduce_fusion.3 = (f32[3,512]{1,0:T(4,128)S(1)}, f32[3,512,2560]{2,1,0:T(8,128)}) fusion(f32[3,512,2560]{2,1,0:T(8,128)S(1)} %fusion.137, f32[3,512]{1,0:T(4,128)S(1)} %dynamic-slice_bitcast_fusion.2, pred[512,2560]{1,0:T(8,128)(4,1)S(1)} %or_and_fusion.5, bf16[2560,3,64]{0,2,1:T(8,128)(2,1)S(1)} %copy-done.12, ...), kind=kOutput, calls=%fused_computation.19.clone.1 | convolution fusion | flops 534772224 | bytes 33959940 | tf_op jit(solution)/shard_map/while/body/eval_jaxpr/qhd,khd->hqk/dot_general | solution.py:101
  611.8 15.2 %subtract_convert_fusion.2 = bf16[3,512,2560]{2,1,0:T(8,128)(2,1)S(1)} fusion(f32[3,512,2560]{2,1,0:T(8,128)} %get-tuple-element.433, f32[3,512,2560]{2,1,0:T(8,128)} %copy-done, f32[3,512]{1,0:T(4,128)S(1)} %get-tuple-element.434, f32[3,512]{1,0:T(4,128)S(1)} %dynamic-slice_bitcast_fusion.2, pred[512,2560]{1,0:T(8,128)(4,1)S(1)} %or_and_fusion.5), kind=kLoop, calls=%fused_computation.18.clone.1 | loop fusion | flops 39321600 | bytes 40644608 | tf_op jit(solution)/shard_map/while/body/eval_jaxpr/convert_element_type | solution.py:105
  632.3 8.7 dynamic_update_slice.23
  647.4 14.4 %fusion.139 = f32[2560,3,64]{0,2,1:T(8,128)} fusion(f32[3,512,2560]{2,1,0:T(8,128)S(1)} %fusion.137, f32[3,512]{1,0:T(4,128)S(1)} %dynamic-slice_bitcast_fusion.2, pred[512,2560]{1,0:T(8,128)(4,1)S(1)} %or_and_fusion.5, f32[2560,3,64]{0,2,1:T(8,128)} %get-tuple-element.492, pred[]{:T(512)S(6)} %compare.3, ...), kind=kOutput, calls=%fused_computation.30.clone.1 | convolution fusion | flops 531824640 | bytes 21174276 | tf_op jit(solution)/shard_map/while/body/eval_jaxpr/hqk,qhd->khd/dot_general | solution.py:98
  661.8 15.0 %multiply_reduce_fusion.3 = (f32[3,512]{1,0:T(4,128)S(1)}, f32[3,512,2560]{2,1,0:T(8,128)}) fusion(f32[3,512,2560]{2,1,0:T(8,128)S(1)} %fusion.137, f32[3,512]{1,0:T(4,128)S(1)} %dynamic-slice_bitcast_fusion.2, pred[512,2560]{1,0:T(8,128)(4,1)S(1)} %or_and_fusion.5, bf16[2560,3,64]{0,2,1:T(8,128)(2,1)S(1)} %copy-done.12, ...), kind=kOutput, calls=%fused_computation.19.clone.1 | convolution fusion | flops 534772224 | bytes 33959940 | tf_op jit(solution)/shard_map/while/body/eval_jaxpr/qhd,khd->hqk/dot_general | solution.py:101
  676.8 15.2 %subtract_convert_fusion.2 = bf16[3,512,2560]{2,1,0:T(8,128)(2,1)S(1)} fusion(f32[3,512,2560]{2,1,0:T(8,128)} %get-tuple-element.433, f32[3,512,2560]{2,1,0:T(8,128)} %copy-done, f32[3,512]{1,0:T(4,128)S(1)} %get-tuple-element.434, f32[3,512]{1,0:T(4,128)S(1)} %dynamic-slice_bitcast_fusion.2, pred[512,2560]{1,0:T(8,128)(4,1)S(1)} %or_and_fusion.5), kind=kLoop, calls=%fused_computation.18.clone.1 | loop fusion | flops 39321600 | bytes 40644608 | tf_op jit(solution)/shard_map/while/body/eval_jaxpr/convert_element_type | solution.py:105
  697.4 8.7 dynamic_update_slice.23
  712.5 14.4 %fusion.139 = f32[2560,3,64]{0,2,1:T(8,128)} fusion(f32[3,512,2560]{2,1,0:T(8,128)S(1)} %fusion.137, f32[3,512]{1,0:T(4,128)S(1)} %dynamic-slice_bitcast_fusion.2, pred[512,2560]{1,0:T(8,128)(4,1)S(1)} %or_and_fusion.5, f32[2560,3,64]{0,2,1:T(8,128)} %get-tuple-element.492, pred[]{:T(512)S(6)} %compare.3, ...), kind=kOutput, calls=%fused_computation.30.clone.1 | convolution fusion | flops 531824640 | bytes 21174276 | tf_op jit(solution)/shard_map/while/body/eval_jaxpr/hqk,qhd->khd/dot_general | solution.py:98
  726.9 15.0 %multiply_reduce_fusion.3 = (f32[3,512]{1,0:T(4,128)S(1)}, f32[3,512,2560]{2,1,0:T(8,128)}) fusion(f32[3,512,2560]{2,1,0:T(8,128)S(1)} %fusion.137, f32[3,512]{1,0:T(4,128)S(1)} %dynamic-slice_bitcast_fusion.2, pred[512,2560]{1,0:T(8,128)(4,1)S(1)} %or_and_fusion.5, bf16[2560,3,64]{0,2,1:T(8,128)(2,1)S(1)} %copy-done.12, ...), kind=kOutput, calls=%fused_computation.19.clone.1 | convolution fusion | flops 534772224 | bytes 33959940 | tf_op jit(solution)/shard_map/while/body/eval_jaxpr/qhd,khd->hqk/dot_general | solution.py:101
  741.9 15.2 %subtract_convert_fusion.2 = bf16[3,512,2560]{2,1,0:T(8,128)(2,1)S(1)} fusion(f32[3,512,2560]{2,1,0:T(8,128)} %get-tuple-element.433, f32[3,512,2560]{2,1,0:T(8,128)} %copy-done, f32[3,512]{1,0:T(4,128)S(1)} %get-tuple-element.434, f32[3,512]{1,0:T(4,128)S(1)} %dynamic-slice_bitcast_fusion.2, pred[512,2560]{1,0:T(8,128)(4,1)S(1)} %or_and_fusion.5), kind=kLoop, calls=%fused_computation.18.clone.1 | loop fusion | flops 39321600 | bytes 40644608 | tf_op jit(solution)/shard_map/while/body/eval_jaxpr/convert_element_type | solution.py:105
  762.5 8.7 dynamic_update_slice.23
  777.6 14.4 %fusion.139 = f32[2560,3,64]{0,2,1:T(8,128)} fusion(f32[3,512,2560]{2,1,0:T(8,128)S(1)} %fusion.137, f32[3,512]{1,0:T(4,128)S(1)} %dynamic-slice_bitcast_fusion.2, pred[512,2560]{1,0:T(8,128)(4,1)S(1)} %or_and_fusion.5, f32[2560,3,64]{0,2,1:T(8,128)} %get-tuple-element.492, pred[]{:T(512)S(6)} %compare.3, ...), kind=kOutput, calls=%fused_computation.30.clone.1 | convolution fusion | flops 531824640 | bytes 21174276 | tf_op jit(solution)/shard_map/while/body/eval_jaxpr/hqk,qhd->khd/dot_general | solution.py:98
  792.0 15.0 %multiply_reduce_fusion.3 = (f32[3,512]{1,0:T(4,128)S(1)}, f32[3,512,2560]{2,1,0:T(8,128)}) fusion(f32[3,512,2560]{2,1,0:T(8,128)S(1)} %fusion.137, f32[3,512]{1,0:T(4,128)S(1)} %dynamic-slice_bitcast_fusion.2, pred[512,2560]{1,0:T(8,128)(4,1)S(1)} %or_and_fusion.5, bf16[2560,3,64]{0,2,1:T(8,128)(2,1)S(1)} %copy-done.12, ...), kind=kOutput, calls=%fused_computation.19.clone.1 | convolution fusion | flops 534772224 | bytes 33959940 | tf_op jit(solution)/shard_map/while/body/eval_jaxpr/qhd,khd->hqk/dot_general | solution.py:101
  807.0 15.2 %subtract_convert_fusion.2 = bf16[3,512,2560]{2,1,0:T(8,128)(2,1)S(1)} fusion(f32[3,512,2560]{2,1,0:T(8,128)} %get-tuple-element.433, f32[3,512,2560]{2,1,0:T(8,128)} %copy-done, f32[3,512]{1,0:T(4,128)S(1)} %get-tuple-element.434, f32[3,512]{1,0:T(4,128)S(1)} %dynamic-slice_bitcast_fusion.2, pred[512,2560]{1,0:T(8,128)(4,1)S(1)} %or_and_fusion.5), kind=kLoop, calls=%fused_computation.18.clone.1 | loop fusion | flops 39321600 | bytes 40644608 | tf_op jit(solution)/shard_map/while/body/eval_jaxpr/convert_element_type | solution.py:105
  827.5 8.7 dynamic_update_slice.23
  843.9 4.8 convolution_convert_fusion.3
  849.9 9.9 convolution_convert_fusion.1
  859.9 8.1 fusion.76
  868.2 9.6 fusion.73
  877.9 7.7 fusion.44
  893.8 37.1 %all-reduce.8 = (f32[768]{0:T(1024)S(1)}, f32[768]{0:T(1024)S(1)}, f32[768]{0:T(1024)S(1)}, f32[768]{0:T(1024)S(1)}) all-reduce(f32[768]{0:T(1024)S(1)} %get-tuple-element.224, f32[768]{0:T(1024)S(1)} %get-tuple-element.229, f32[768]{0:T(1024)S(1)} %copy-done.34, ...), channel_id=10, replica_groups=mesh['dp'=8,'tensor'=4] {'dp'}, use_global_device_ids=true, to_apply=%region_26.27.clone | all-reduce | flops 3072 | bytes 24576
  931.2 6.4 all-reduce.9
  937.7 4.1 fusion.61
  941.8 68.8 %reduce-scatter.21.cloned.1.call-done = f32[96,768]{1,0:T(8,128)} async-done(((f32[768,768]{1,0:T(8,128)}), f32[96,768]{1,0:T(8,128)}) %reduce-scatter.21.cloned.1.call-update) | async-done | bytes 294928 | tf_op jit(solution)/shard_map/reduce_scatter | solution.py:216
  1010.6 73.1 %reduce-scatter.23.cloned.1.call-done = f32[768,96]{0,1:T(8,128)} async-done(((f32[768,768]{0,1:T(8,128)}), f32[768,96]{0,1:T(8,128)}) %reduce-scatter.23.cloned.1.call-update) | async-done | bytes 294928 | tf_op jit(solution)/shard_map/reduce_scatter | solution.py:217
  1083.8 73.1 %reduce-scatter.19.cloned.1.call-done = f32[96,3,192]{2,0,1:T(8,128)} async-done(((f32[768,3,192]{2,0,1:T(8,128)}), f32[96,3,192]{2,0,1:T(8,128)}) %reduce-scatter.19.cloned.1.call-update) | async-done | bytes 221200 | tf_op jit(solution)/shard_map/reduce_scatter | solution.py:214
  (284 shorter events, 115.3 us)
Async XLA Ops:
  8.0 35.1 %copy-start.40 = (s32[1,8]{1,0:T(1,128)S(1)}, s32[1,8]{1,0:T(1,128)}, u32[]{:S(2)}) copy-start(s32[1,8]{1,0:T(1,128)} %param.17) | copy-start | bytes 100
  8.0 35.3 %copy-start.29 = (bf16[192,96]{1,0:T(8,128)(2,1)S(1)}, bf16[192,96]{1,0:T(8,128)(2,1)}, u32[]{:S(2)}) copy-start(bf16[192,96]{1,0:T(8,128)(2,1)} %param.19) | copy-start | bytes 110596
  8.0 35.4 %copy-start.16 = (bf16[96,3,192]{2,0,1:T(8,128)(2,1)S(1)}, bf16[96,3,192]{2,0,1:T(8,128)(2,1)}, u32[]{:S(2)}) copy-start(bf16[96,3,192]{2,0,1:T(8,128)(2,1)} %param.18) | copy-start | bytes 331780
  8.0 105.7 %all-gather.7.cloned.1.call-start = ((), (), s32[]{:S(2)}) async-start(), calls=%async_computation.8 | async-start | bytes 4915200 | tf_op jit(solution)/shard_map/all_gather | solution.py:153
  37.4 5.9 copy-start.25
  38.8 4.5 copy-start.19
  40.4 2.9 copy-start.27
  43.0 246.5 %reduce-scatter.11.cloned.1.call-start = ((), (), s32[]{:S(2)}) async-start(), calls=%async_computation.9 | async-start | bytes 4915200 | tf_op jit(solution)/shard_map/reduce_scatter | solution.py:161
  80.0 38.3 %copy-start.14 = (bf16[768,3,192]{0,2,1:T(8,128)(2,1)}, bf16[768,3,192]{0,2,1:T(8,128)(2,1)S(1)}, u32[]{:S(2)}) copy-start(bf16[768,3,192]{0,2,1:T(8,128)(2,1)S(1)} %copy.33) | copy-start | bytes 2654212
  241.8 2.0 copy-start.9
  246.9 1.8 copy-start.36
  246.9 42.6 %copy-start.1 = (bf16[640,768]{1,0:T(8,128)(2,1)S(1)}, bf16[640,768]{1,0:T(8,128)(2,1)}, u32[]{:S(2)}) copy-start(bf16[640,768]{1,0:T(8,128)(2,1)} %param.15) | copy-start | bytes 2949124
  247.0 47.5 %all-gather.13.cloned.1.call-start = ((), (), s32[]{:S(2)}) async-start(), calls=%async_computation.12 | async-start | bytes 1327104 | tf_op jit(solution)/shard_map/all_gather | solution.py:135
  247.5 75.7 %all-gather.15.cloned.1.call-start = ((), (), s32[]{:S(2)}) async-start(), calls=%async_computation.14 | async-start | bytes 4915200 | tf_op jit(solution)/shard_map/all_gather | solution.py:181
  248.1 118.6 %all-gather.11.cloned.1.call-start = ((), (), s32[]{:S(2)}) async-start(), calls=%async_computation.11 | async-start | bytes 1327104 | tf_op jit(solution)/shard_map/all_gather | solution.py:134
  248.7 151.4 %all-gather.9.cloned.1.call-start = ((), (), s32[]{:S(2)}) async-start(), calls=%async_computation.10 | async-start | bytes 4915200 | tf_op jit(solution)/shard_map/all_gather | solution.py:169
  248.8 217.6 %copy-start.21 = (f32[768]{0:T(1024)}, f32[768]{0:T(1024)S(1)}, u32[]{:S(2)}) copy-start(f32[768]{0:T(1024)S(1)} %convert_element_type.109) | copy-start | bytes 9220
  289.5 3.3 copy-start.5
  291.2 175.2 %copy-start.17 = (f32[640]{0:T(1024)}, f32[640]{0:T(1024)S(1)}, u32[]{:S(2)}) copy-start(f32[640]{0:T(1024)S(1)} %broadcast_multiply_fusion.4) | copy-start | bytes 7684
  292.9 173.5 %copy-start.23 = (f32[640]{0:T(1024)}, f32[640]{0:T(1024)S(1)}, u32[]{:S(2)}) copy-start(f32[640]{0:T(1024)S(1)} %add_rsqrt_fusion) | copy-start | bytes 7684
  294.4 169.2 %reduce-scatter.15.cloned.1.call-start = ((), (), s32[]{:S(2)}) async-start(), calls=%async_computation.15 | async-start | bytes 4915200 | tf_op jit(solution)/shard_map/reduce_scatter | solution.py:187
  400.1 15.6 %copy-start.39 = (bf16[768,768]{1,0:T(8,128)(2,1)S(1)}, bf16[768,768]{1,0:T(8,128)(2,1)}, u32[]{:S(2)}) copy-start(bf16[768,768]{1,0:T(8,128)(2,1)} %all-gather.11.cloned.1.call-done) | copy-start | bytes 3538948
  413.8 2.0 copy-start.41
  420.5 82.9 %all-gather.17.cloned.1.call-start = ((), (), s32[]{:S(2)}) async-start(), calls=%async_computation.16 | async-start | bytes 4915200 | tf_op jit(solution)/shard_map/all_gather | solution.py:194
  470.4 416.2 %reduce-scatter.25.cloned.1.call-start = ((), (), s32[]{:S(2)}) async-start(), calls=%async_computation.21 | async-start | bytes 884736
  508.3 383.3 %reduce-scatter.17.cloned.1.call-start = ((), (), s32[]{:S(2)}) async-start(), calls=%async_computation.17 | async-start | bytes 4915200 | tf_op jit(solution)/shard_map/reduce_scatter | solution.py:207
  519.5 12.2 %copy-start = (f32[3,512,2560]{2,1,0:T(8,128)}, f32[3,512,2560]{2,1,0:T(8,128)S(1)}, u32[]{:S(2)}) copy-start(f32[3,512,2560]{2,1,0:T(8,128)S(1)} %fusion.137) | copy-start | bytes 47185924 | tf_op jit(solution)/shard_map/while
  519.5 12.2 %copy-start.12 = (bf16[2560,3,64]{0,2,1:T(8,128)(2,1)S(1)}, bf16[2560,3,64]{0,2,1:T(8,128)(2,1)}, u32[]{:S(2)}) copy-start(bf16[2560,3,64]{0,2,1:T(8,128)(2,1)} %get-tuple-element.517) | copy-start | bytes 2949124 | tf_op jit(solution)/shard_map/while
  562.0 2.5 copy-start.3
  567.0 9.0 copy-start.4
  582.4 14.4 %copy-start = (f32[3,512,2560]{2,1,0:T(8,128)}, f32[3,512,2560]{2,1,0:T(8,128)S(1)}, u32[]{:S(2)}) copy-start(f32[3,512,2560]{2,1,0:T(8,128)S(1)} %fusion.137) | copy-start | bytes 47185924 | tf_op jit(solution)/shard_map/while
  582.4 14.4 %copy-start.12 = (bf16[2560,3,64]{0,2,1:T(8,128)(2,1)S(1)}, bf16[2560,3,64]{0,2,1:T(8,128)(2,1)}, u32[]{:S(2)}) copy-start(bf16[2560,3,64]{0,2,1:T(8,128)(2,1)} %get-tuple-element.517) | copy-start | bytes 2949124 | tf_op jit(solution)/shard_map/while
  627.0 2.5 copy-start.3
  632.0 9.0 copy-start.4
  647.4 14.4 %copy-start = (f32[3,512,2560]{2,1,0:T(8,128)}, f32[3,512,2560]{2,1,0:T(8,128)S(1)}, u32[]{:S(2)}) copy-start(f32[3,512,2560]{2,1,0:T(8,128)S(1)} %fusion.137) | copy-start | bytes 47185924 | tf_op jit(solution)/shard_map/while
  647.4 14.4 %copy-start.12 = (bf16[2560,3,64]{0,2,1:T(8,128)(2,1)S(1)}, bf16[2560,3,64]{0,2,1:T(8,128)(2,1)}, u32[]{:S(2)}) copy-start(bf16[2560,3,64]{0,2,1:T(8,128)(2,1)} %get-tuple-element.517) | copy-start | bytes 2949124 | tf_op jit(solution)/shard_map/while
  692.1 2.5 copy-start.3
  697.1 9.0 copy-start.4
  712.5 14.4 %copy-start = (f32[3,512,2560]{2,1,0:T(8,128)}, f32[3,512,2560]{2,1,0:T(8,128)S(1)}, u32[]{:S(2)}) copy-start(f32[3,512,2560]{2,1,0:T(8,128)S(1)} %fusion.137) | copy-start | bytes 47185924 | tf_op jit(solution)/shard_map/while
  712.5 14.4 %copy-start.12 = (bf16[2560,3,64]{0,2,1:T(8,128)(2,1)S(1)}, bf16[2560,3,64]{0,2,1:T(8,128)(2,1)}, u32[]{:S(2)}) copy-start(bf16[2560,3,64]{0,2,1:T(8,128)(2,1)} %get-tuple-element.517) | copy-start | bytes 2949124 | tf_op jit(solution)/shard_map/while
  757.1 2.5 copy-start.3
  762.2 9.0 copy-start.4
  777.6 14.4 %copy-start = (f32[3,512,2560]{2,1,0:T(8,128)}, f32[3,512,2560]{2,1,0:T(8,128)S(1)}, u32[]{:S(2)}) copy-start(f32[3,512,2560]{2,1,0:T(8,128)S(1)} %fusion.137) | copy-start | bytes 47185924 | tf_op jit(solution)/shard_map/while
  777.6 14.4 %copy-start.12 = (bf16[2560,3,64]{0,2,1:T(8,128)(2,1)S(1)}, bf16[2560,3,64]{0,2,1:T(8,128)(2,1)}, u32[]{:S(2)}) copy-start(bf16[2560,3,64]{0,2,1:T(8,128)(2,1)} %get-tuple-element.517) | copy-start | bytes 2949124 | tf_op jit(solution)/shard_map/while
  822.2 2.5 copy-start.3
  827.2 9.0 copy-start.4
  839.4 4.5 copy-start.15
  848.7 88.9 %reduce-scatter.13.cloned.1.call-start = ((), (), s32[]{:S(2)}) async-start(), calls=%async_computation.13 | async-start | bytes 4915200 | tf_op jit(solution)/shard_map/reduce_scatter | solution.py:174
  859.8 150.8 %reduce-scatter.21.cloned.1.call-start = ((), (), s32[]{:S(2)}) async-start(), calls=%async_computation.19 | async-start | bytes 2654208 | tf_op jit(solution)/shard_map/reduce_scatter | solution.py:216
  868.0 215.8 %reduce-scatter.23.cloned.1.call-start = ((), (), s32[]{:S(2)}) async-start(), calls=%async_computation.20 | async-start | bytes 2654208 | tf_op jit(solution)/shard_map/reduce_scatter | solution.py:217
  877.8 279.1 %reduce-scatter.19.cloned.1.call-start = ((), (), s32[]{:S(2)}) async-start(), calls=%async_computation.18 | async-start | bytes 2654208 | tf_op jit(solution)/shard_map/reduce_scatter | solution.py:214
  877.9 13.7 %copy-start.2 = (bf16[640,768]{1,0:T(8,128)(2,1)S(1)}, bf16[640,768]{1,0:T(8,128)(2,1)}, u32[]{:S(2)}) copy-start(bf16[640,768]{1,0:T(8,128)(2,1)} %param.15) | copy-start | bytes 2949124
  877.9 13.7 %copy-start.20 = (f32[640]{0:T(1024)S(1)}, f32[640]{0:T(1024)}, u32[]{:S(2)}) copy-start(f32[640]{0:T(1024)} %copy-done.19) | copy-start | bytes 7684
  877.9 13.7 %copy-start.26 = (f32[768]{0:T(1024)S(1)}, f32[768]{0:T(1024)}, u32[]{:S(2)}) copy-start(f32[768]{0:T(1024)} %copy-done.25) | copy-start | bytes 9220
  877.9 13.7 %copy-start.28 = (f32[640]{0:T(1024)S(1)}, f32[640]{0:T(1024)}, u32[]{:S(2)}) copy-start(f32[640]{0:T(1024)} %copy-done.27) | copy-start | bytes 7684
  885.7 8.1 copy-start.34
  885.7 8.1 copy-start.35
  885.7 51.9 %copy-start.6 = (bf16[640,768]{1,0:T(8,128)(2,1)S(1)}, bf16[640,768]{1,0:T(8,128)(2,1)}, u32[]{:S(2)}) copy-start(bf16[640,768]{1,0:T(8,128)(2,1)} %reduce-scatter.11.cloned.1.call-done) | copy-start | bytes 2949124
  885.7 51.9 %copy-start.7 = (bf16[640,768]{1,0:T(8,128)(2,1)S(1)}, bf16[640,768]{1,0:T(8,128)(2,1)}, u32[]{:S(2)}) copy-start(bf16[640,768]{1,0:T(8,128)(2,1)} %param.16) | copy-start | bytes 2949124
  885.7 51.9 %copy-start.18 = (f32[640]{0:T(1024)S(1)}, f32[640]{0:T(1024)}, u32[]{:S(2)}) copy-start(f32[640]{0:T(1024)} %copy-done.17) | copy-start | bytes 7684
  885.7 51.9 %copy-start.22 = (f32[768]{0:T(1024)S(1)}, f32[768]{0:T(1024)}, u32[]{:S(2)}) copy-start(f32[768]{0:T(1024)} %copy-done.21) | copy-start | bytes 9220
  885.7 51.9 %copy-start.24 = (f32[640]{0:T(1024)S(1)}, f32[640]{0:T(1024)}, u32[]{:S(2)}) copy-start(f32[640]{0:T(1024)} %copy-done.23) | copy-start | bytes 7684
  885.7 51.9 %copy-start.31 = (f32[640]{0:T(1024)S(1)}, f32[640]{0:T(1024)}, u32[]{:S(2)}) copy-start(f32[640]{0:T(1024)} %copy-done.30) | copy-start | bytes 7684
  885.7 51.9 %copy-start.33 = (f32[640]{0:T(1024)S(1)}, f32[640]{0:T(1024)}, u32[]{:S(2)}) copy-start(f32[640]{0:T(1024)} %copy-done.32) | copy-start | bytes 7684
  (8 other events, 9.4 us)
Sparse Core Ops, SparseCore 0:
  43.1 30.2 all-gather.6
  247.1 42.4 reduce-scatter.10
  420.6 42.8 reduce-scatter.14
Sparse Core Ops, SparseCore 1:
  249.6 40.9 all-gather.12
  292.0 31.2 all-gather.14
  325.3 41.4 all-gather.10
  368.9 31.2 all-gather.8
  470.5 32.8 all-gather.16
  508.4 63.3 reduce-scatter.24
  848.7 42.8 reduce-scatter.16
  894.0 42.8 reduce-scatter.12
  940.8 69.8 reduce-scatter.20
  1014.7 69.0 reduce-scatter.22
  1087.7 69.1 reduce-scatter.18
where the time goes:
time: 1170 us; the launch traced here: 1160 us
  waiting for transfers between devices  433 us (37%)
  matrix products  348 us (30%)
  other arithmetic  148 us (13%)
  blocking collectives  137 us (12%)
  local copies, waits for them, and re-layouts  71.7 us (6%)
  between operations  17.7 us (2%)
    convert_element_type x5, other arithmetic, step(): score_grad = (prob * weight_grad - signed * inner).astype(jnp.bfloat16)  76.2 us
    dot_general x5, matrix products, step(): jnp.einsum('qhd,khd->hqk', grad_block, values, preferred_element_type=jnp...  75 us
    reduce_scatter x1, waiting for transfers between devices, on_device(): lax.psum_scatter(qkv_grad, 'dp', scatter_dimension=0, tiled=True)  73.1 us
    reduce_scatter x1, waiting for transfers between devices, on_device(): lax.psum_scatter(proj_grad, 'dp', scatter_dimension=1, tiled=True)  73.1 us
    dot_general x5, matrix products, step(): jnp.einsum('hqk,qhd->khd', rounded, grad_block, preferred_element_type=jn...  69.8 us
    reduce_scatter x1, waiting for transfers between devices, on_device(): lax.psum_scatter(fc_grad, 'dp', scatter_dimension=0, tiled=True)  68.8 us
    unnamed x2, blocking collectives  61 us
    dot_general x5, matrix products, one(): jnp.einsum('hqk,khd->qhd', weights, values, preferred_element_type=jnp.fl...  52.9 us
  transfers between devices with their start and end apart: 14, of which 10 were waited for; matrix products, arithmetic and copies ran while one was open for 34% of the time, Pallas kernels for 0%

commit v1 on v0

--- a/solution.py
+++ b/solution.py
@@ -1,10 +1,241 @@
+import functools
+
 import jax
 import jax.numpy as jnp
 from jax import lax
+from jax.experimental import pallas as pl
+from jax.experimental.pallas import tpu as pltpu
 from jax.sharding import PartitionSpec as P
 
 HEAD = 64
 PROMPT = 512
+TILE = 256
+REACH = 2
+BIG = 3.0e38
+
+
+def nt(left, right):
+    return lax.dot_general(left, right, (((1,), (1,)), ((), ())), preferred_element_type=jnp.float32)
+
+
+def nn(left, right):
+    return jnp.dot(left, right, preferred_element_type=jnp.float32)
+
+
+def first_of(lengths_ref, total):
+    places = lax.broadcasted_iota(jnp.int32, (1, total), 1)
+    first = jnp.zeros((1, total), jnp.int32)
+    begin = jnp.int32(PROMPT)
+    for c in range(lengths_ref.shape[1]):
+        first = jnp.where(places >= begin, begin, first)
+        begin = begin + lengths_ref[0, c]
+    return first
+
+
+def key_parts(index):
+    if isinstance(index, int) and index < PROMPT // TILE:
+        return [(j * TILE, j == index, False) for j in range(index + 1)]
+    parts = [(j * TILE, False, False) for j in range(PROMPT // TILE)]
+    if isinstance(index, int):
+        band = range(max(PROMPT // TILE, index - REACH), index + 1)
+        return parts + [(j * TILE, j == index, True) for j in band]
+    return parts + [((index - r) * TILE, r == 0, True) for r in range(REACH, -1, -1)]
+
+
+def seen(key0, query0, first, diagonal, banded):
+    keys = key0 + lax.broadcasted_iota(jnp.int32, (TILE, TILE), 0)
+    mask = None
+    if banded:
+        mask = keys >= first
+    if diagonal:
+        causal = keys <= query0 + lax.broadcasted_iota(jnp.int32, (TILE, TILE), 1)
+        mask = causal if mask is None else mask & causal
+    return mask
+
+
+def rows(ref, start):
+    return ref[pl.ds(start if isinstance(start, int) else pl.multiple_of(start, TILE), TILE), :]
+
+
+def cols(ref, start):
+    return ref[:, pl.ds(start if isinstance(start, int) else pl.multiple_of(start, TILE), TILE)]
+
+
+def signs(values):
+    return jnp.clip(values * BIG, -1.0, 1.0)
+
+
+def each_tile(count, body):
+    steady = PROMPT // TILE + REACH
+    for index in range(min(steady, count)):
+        body(index)
+    if count > steady:
+        lax.fori_loop(steady, count, lambda i, c: (body(i), c)[1], 0)
+
+
+def forward_kernel(heads, lengths_ref, qkv_ref, mixed_ref, lse_ref, q_s, k_s, vt_s, o_s, first_s):
+    total = qkv_ref.shape[0]
+    local = heads * HEAD
+    head = pl.program_id(0)
+
+    @pl.when(head == 0)
+    def _():
+        first_s[...] = first_of(lengths_ref, total)
+
+    for h in range(heads):
+        @pl.when(head == h)
+        def _(h=h):
+            at = h * HEAD
+            q_s[...] = qkv_ref[:, at : at + HEAD] * jnp.bfloat16(HEAD**-0.5)
+            k_s[...] = qkv_ref[:, local + at : local + at + HEAD]
+            vt_s[...] = qkv_ref[:, 2 * local + at : 2 * local + at + HEAD].T
+
+    def body(index):
+        query0 = index * TILE
+        query = rows(q_s, query0)
+        first = cols(first_s, query0)
+        raws, sizes, tops = [], [], []
+        parts = key_parts(index)
+        for key0, diagonal, banded in parts:
+            raw = nt(rows(k_s, key0), query)
+            size = jnp.abs(raw)
+            mask = seen(key0, query0, first, diagonal, banded)
+            if mask is not None:
+                size = jnp.where(mask, size, -1e30)
+            raws.append(raw)
+            sizes.append(size)
+            tops.append(jnp.max(size, axis=0, keepdims=True))
+        top = functools.reduce(jnp.maximum, tops)
+        expos = [jnp.exp(size - top) for size in sizes]
+        total_e = functools.reduce(jnp.add, [jnp.sum(e, axis=0, keepdims=True) for e in expos])
+        inverse = 1.0 / total_e
+        acc = None
+        for (key0, _, _), raw, expo in zip(parts, raws, expos):
+            weight = (signs(raw) * (expo * inverse)).astype(jnp.bfloat16)
+            term = nn(cols(vt_s, key0), weight)
+            acc = term if acc is None else acc + term
+        o_s[pl.ds(query0, TILE), :] = acc.T.astype(jnp.bfloat16)
+        lse_ref[0, :, pl.ds(query0, TILE)] = top + jnp.log(total_e)
+
+    each_tile(total // TILE, body)
+    for h in range(heads):
+        @pl.when(head == h)
+        def _(h=h):
+            mixed_ref[:, h * HEAD : (h + 1) * HEAD] = o_s[...]
+
+
+def whole(shape):
+    return pl.BlockSpec(shape, lambda *_: (0,) * len(shape), pipeline_mode=pl.Buffered(1))
+
+
+def attend(qkv, lengths, heads):
+    total = qkv.shape[0]
+    return pl.pallas_call(
+        functools.partial(forward_kernel, heads),
+        grid=(heads,),
+        in_specs=[pl.BlockSpec(memory_space=pltpu.SMEM), whole(qkv.shape)],
+        out_specs=[whole((total, heads * HEAD)), pl.BlockSpec((1, 1, total), lambda h: (h, 0, 0))],
+        out_shape=[
+            jax.ShapeDtypeStruct((total, heads * HEAD), jnp.bfloat16),
+            jax.ShapeDtypeStruct((heads, 1, total), jnp.float32),
+        ],
+        scratch_shapes=[
+            pltpu.VMEM((total, HEAD), jnp.bfloat16),
+            pltpu.VMEM((total, HEAD), jnp.bfloat16),
+            pltpu.VMEM((HEAD, total), jnp.bfloat16),
+            pltpu.VMEM((total, HEAD), jnp.bfloat16),
+            pltpu.VMEM((1, total), jnp.int32),
+        ],
+        compiler_params=pltpu.CompilerParams(vmem_limit_bytes=48 << 20),
+        name="attend",
+    )(lengths, qkv)
+
+
+def backward_kernel(
+    heads, lengths_ref, qkv_ref, mixed_ref, dmix_ref, lse_ref, grad_ref,
+    q_s, k_s, kt_s, v_s, d_s, delta_s, dq_s, dk_s, dv_s, first_s,
+):
+    total = qkv_ref.shape[0]
+    local = heads * HEAD
+    head = pl.program_id(0)
+    scale = HEAD**-0.5
+
+    @pl.when(head == 0)
+    def _():
+        first_s[...] = first_of(lengths_ref, total)
+
+    for h in range(heads):
+        @pl.when(head == h)
+        def _(h=h):
+            at = h * HEAD
+            q_s[...] = qkv_ref[:, at : at + HEAD] * jnp.bfloat16(scale)
+            key = qkv_ref[:, local + at : local + at + HEAD]
+            k_s[...] = key
+            kt_s[...] = key.T
+            v_s[...] = qkv_ref[:, 2 * local + at : 2 * local + at + HEAD]
+            grad = dmix_ref[:, at : at + HEAD]
+            d_s[...] = grad
+            product = grad.astype(jnp.float32) * mixed_ref[:, at : at + HEAD].astype(jnp.float32)
+            delta_s[...] = jnp.sum(product.T, axis=0, keepdims=True)
+
+    dk_s[...] = jnp.zeros_like(dk_s)
+    dv_s[...] = jnp.zeros_like(dv_s)
+
+    def body(index):
+        query0 = index * TILE
+        query = rows(q_s, query0)
+        grad = rows(d_s, query0)
+        first = cols(first_s, query0)
+        lse = lse_ref[0, :, pl.ds(query0, TILE)]
+        inner = cols(delta_s, query0)
+        acc = None
+        for key0, diagonal, banded in key_parts(index):
+            raw = nt(rows(k_s, key0), query)
+            prob = jnp.exp(jnp.abs(raw) - lse)
+            mask = seen(key0, query0, first, diagonal, banded)
+            if mask is not None:
+                prob = jnp.where(mask, prob, 0.0)
+            signed = signs(raw) * prob
+            wgrad = nt(rows(v_s, key0), grad)
+            sgrad = (prob * wgrad - signed * inner).astype(jnp.bfloat16)
+            at = pl.ds(key0, TILE)
+            dv_s[at, :] = dv_s[at, :] + nn(signed.astype(jnp.bfloat16), grad)
+            dk_s[at, :] = dk_s[at, :] + nn(sgrad, query)
+            term = nn(cols(kt_s, key0), sgrad)
+            acc = term if acc is None else acc + term
+        dq_s[pl.ds(query0, TILE), :] = (acc * scale).T.astype(jnp.bfloat16)
+
+    each_tile(total // TILE, body)
+    for h in range(heads):
+        @pl.when(head == h)
+        def _(h=h):
+            at = h * HEAD
+            grad_ref[:, at : at + HEAD] = dq_s[...]
+            grad_ref[:, local + at : local + at + HEAD] = dk_s[...].astype(jnp.bfloat16)
+            grad_ref[:, 2 * local + at : 2 * local + at + HEAD] = dv_s[...].astype(jnp.bfloat16)
+
+
+def attend_back(qkv, mixed, dmix, lse, lengths, heads):
+    total = qkv.shape[0]
+    low = jnp.bfloat16
+    return pl.pallas_call(
+        functools.partial(backward_kernel, heads),
+        grid=(heads,),
+        in_specs=[
+            pl.BlockSpec(memory_space=pltpu.SMEM), whole(qkv.shape), whole(mixed.shape), whole(dmix.shape),
+            pl.BlockSpec((1, 1, total), lambda h: (h, 0, 0)),
+        ],
+        out_specs=whole(qkv.shape),
+        out_shape=jax.ShapeDtypeStruct(qkv.shape, low),
+        scratch_shapes=[
+            pltpu.VMEM((total, HEAD), low), pltpu.VMEM((total, HEAD), low), pltpu.VMEM((HEAD, total), low),
+            pltpu.VMEM((total, HEAD), low), pltpu.VMEM((total, HEAD), low), pltpu.VMEM((1, total), jnp.float32),
+            pltpu.VMEM((total, HEAD), low), pltpu.VMEM((total, HEAD), jnp.float32),
+            pltpu.VMEM((total, HEAD), jnp.float32), pltpu.VMEM((1, total), jnp.int32),
+        ],
+        compiler_params=pltpu.CompilerParams(vmem_limit_bytes=48 << 20),
+        name="attend_back",
+    )(lengths, qkv, mixed, dmix, lse)
 
 
 def normalize(values):
@@ -38,95 +269,11 @@
     )
 
 
-def segment_ids(lengths, total):
-    ends = PROMPT + jnp.cumsum(lengths[0])
-    places = jnp.arange(total, dtype=jnp.int32)
-    passed = jnp.sum((places[:, None] >= ends[None, :]).astype(jnp.int32), axis=1)
-    return (places, jnp.where(places < PROMPT, -1, passed))
-
-
-def visible(query_pos, query_seg, key_pos, key_seg):
-    causal = key_pos[None, :] <= query_pos[:, None]
-    shared = (key_seg[None, :] < 0) | (key_seg[None, :] == query_seg[:, None])
-    return (causal & shared)[None]
-
-
-def attend(queries, keys, values, places, segs, block, scale):
-    count = queries.shape[0] // block
-
-    def one(index):
-        start = index * block
-        query = lax.dynamic_slice_in_dim(queries, start, block, 0)
-        mask = visible(
-            lax.dynamic_slice_in_dim(places, start, block, 0),
-            lax.dynamic_slice_in_dim(segs, start, block, 0),
-            places,
-            segs,
-        )
-        raw = jnp.einsum("qhd,khd->hqk", query, keys, preferred_element_type=jnp.float32) * scale
-        magnitude = jnp.where(mask, jnp.abs(raw), -1e30)
-        top = jnp.max(magnitude, axis=-1, keepdims=True)
-        expo = jnp.where(mask, jnp.exp(magnitude - top), 0.0)
-        total = jnp.sum(expo, axis=-1, keepdims=True)
-        weights = (jnp.sign(raw) * (expo / total)).astype(jnp.bfloat16)
-        mixed = jnp.einsum("hqk,khd->qhd", weights, values, preferred_element_type=jnp.float32)
-        return (mixed.astype(jnp.bfloat16), (top + jnp.log(total))[..., 0])
-
-    mixed, sums = lax.map(one, jnp.arange(count, dtype=jnp.int32))
-    return (mixed.reshape(queries.shape[0], -1), sums)
-
-
-def attend_back(queries, keys, values, grad_mixed, sums, places, segs, block, scale):
-    count = queries.shape[0] // block
-
-    def step(carry, inputs):
-        key_grad, value_grad = carry
-        index, lse_block = inputs
-        start = index * block
-        query = lax.dynamic_slice_in_dim(queries, start, block, 0)
-        grad_block = lax.dynamic_slice_in_dim(grad_mixed, start, block, 0)
-        mask = visible(
-            lax.dynamic_slice_in_dim(places, start, block, 0),
-            lax.dynamic_slice_in_dim(segs, start, block, 0),
-            places,
-            segs,
-        )
-        raw = jnp.einsum("qhd,khd->hqk", query, keys, preferred_element_type=jnp.float32) * scale
-        prob = jnp.where(mask, jnp.exp(jnp.abs(raw) - lse_block[..., None]), 0.0)
-        signed = jnp.sign(raw) * prob
-        rounded = signed.astype(jnp.bfloat16)
-        value_grad = value_grad + jnp.einsum(
-            "hqk,qhd->khd", rounded, grad_block, preferred_element_type=jnp.float32
-        )
-        weight_grad = jnp.einsum(
-            "qhd,khd->hqk", grad_block, values, preferred_element_type=jnp.float32
-        )
-        inner = jnp.sum(signed * weight_grad, axis=-1, keepdims=True)
-        score_grad = (prob * weight_grad - signed * inner).astype(jnp.bfloat16)
-        query_grad = (
-            jnp.einsum("hqk,khd->qhd", score_grad, keys, preferred_element_type=jnp.float32) * scale
-        )
-        key_grad = (
-            key_grad
-            + jnp.einsum("hqk,qhd->khd", score_grad, query, preferred_element_type=jnp.float32)
-            * scale
-        )
-        return ((key_grad, value_grad), query_grad)
-
-    zeros = jnp.zeros(keys.shape, jnp.float32)
-    (key_grad, value_grad), query_grad = lax.scan(
-        step, (zeros, zeros), (jnp.arange(count, dtype=jnp.int32), sums)
-    )
-    return (query_grad.reshape(keys.shape), key_grad, value_grad)
-
-
 def on_device(
     tokens, cotangent, lengths, w_qkv, w_out, w_fc, w_proj, ln1_gain, ln1_bias, ln2_gain, ln2_bias
 ):
     rows = tokens.shape[0]
     group = rows * lax.axis_size("tensor")
-    block = group // max(1, group // 512)
-    scale = HEAD ** (-0.5)
     pieces = (w_qkv, w_out, w_fc, w_proj, ln1_gain, ln1_bias, ln2_gain, ln2_bias)
     qkv_full, out_full, fc_full, proj_full, gain1, bias1, gain2, bias2 = (
         lax.all_gather(pieces[0], "dp", axis=0, tiled=True),
@@ -146,17 +293,12 @@
     local = qkv_full.shape[2]
     heads = local // HEAD
     qkv_mat = qkv_full.reshape(width, 3 * local)
-    places, segs = segment_ids(lengths, group)
     inputs = tokens.astype(jnp.float32)
     normed1, factor1 = normalize(inputs)
     lowered1 = (normed1 * gain1 + bias1).astype(jnp.bfloat16)
     all_norm1 = lax.all_gather(lowered1, "tensor", axis=0, tiled=True)
     projected = jnp.dot(all_norm1, qkv_mat, preferred_element_type=jnp.float32).astype(jnp.bfloat16)
-    projected = projected.reshape(group, 3, heads, HEAD)
-    queries = projected[:, 0]
-    keys = projected[:, 1]
-    values = projected[:, 2]
-    mixed, sums = attend(queries, keys, values, places, segs, block, scale)
+    mixed, sums = attend(projected, lengths, heads)
     part = mixed
     resid = inputs + lax.psum_scatter(
         jnp.dot(part, out_full, preferred_element_type=jnp.float32).astype(jnp.bfloat16),
@@ -193,15 +335,8 @@
     resid_low = resid_grad.astype(jnp.bfloat16)
     resid_all = lax.all_gather(resid_low, "tensor", axis=0, tiled=True)
     out_grad = inner_rows(mixed, resid_all)
-    mixed_grad = times_trans(resid_all, out_full).astype(jnp.bfloat16).reshape(group, heads, HEAD)
-    query_grad, key_grad, value_grad = attend_back(
-        queries, keys, values, mixed_grad, sums, places, segs, block, scale
-    )
-    qkv_grad_low = (
-        jnp.stack([query_grad, key_grad, value_grad], axis=1)
-        .astype(jnp.bfloat16)
-        .reshape(group, 3 * local)
-    )
+    mixed_grad = times_trans(resid_all, out_full).astype(jnp.bfloat16)
+    qkv_grad_low = attend_back(projected, mixed, mixed_grad, sums, lengths, heads)
     qkv_grad = inner_rows(all_norm1, qkv_grad_low).reshape(width, 3, local)
     part = qkv_grad_low
     norm1_grad = lax.psum_scatter(

time: 1170 us -> 799 us (0.68)
  matrix products: 348 us -> 83 us
  other arithmetic: 148 us -> 20 us
  Pallas kernels: 0 us -> 79.2 us
  local copies, waits for them, and re-layouts: 71.7 us -> 18.9 us
    dot_general x35 -> x0, matrix products: 264 us -> none  [the longest x5 75 us: step(): jnp.einsum('qhd,khd->hqk', grad_block, values, preferred_element_type=jnp...]
    pallas_call x0 -> x2, Pallas kernels: none -> 79.2 us  [the longest x1 44.8 us: attend_back(): pl.pallas_call(functools.partial(backward_kernel, heads), grid=(heads,),...]
    convert_element_type x6 -> x0, other arithmetic: 79 us -> none  [the longest x5 76.2 us: step(): score_grad = (prob * weight_grad - signed * inner).astype(jnp.bfloat16)]
    dynamic_update_slice x10 -> x0, local copies, waits for them, and re-layouts: 44.8 us -> none  [attend_back(): lax.scan(step, (zeros, zeros), (jnp.arange(count, dtype=jnp.int32), sums))]
    reduce_sum x6 -> x0, other arithmetic: 27.4 us -> none  [the longest x5 27.3 us: one(): total = jnp.sum(expo, axis=-1, keepdims=True)]
    and x10 -> x0, other arithmetic: 18.2 us -> none  [visible(): return (causal & shared)[None]]
  transfers between devices with their start and end apart: 14 -> 14, of which waited for: 10 -> 10; matrix products, arithmetic and copies ran while one was open for 34% -> 9% of each run, Pallas kernels for 0% -> 6%
where the time goes in v1:
time: 799 us; the launch traced here: 796 us
  waiting for transfers between devices  440 us (55%)
  blocking collectives  136 us (17%)
  matrix products  83 us (10%)
  Pallas kernels  79.2 us (10%)
  other arithmetic  20 us (3%)
  local copies, waits for them, and re-layouts  18.9 us (2%)
  between operations  17.5 us (2%)
    reduce_scatter x1, waiting for transfers between devices, on_device(): lax.psum_scatter(proj_grad, 'dp', scatter_dimension=1, tiled=True)  73.1 us
    reduce_scatter x1, waiting for transfers between devices, on_device(): lax.psum_scatter(qkv_grad, 'dp', scatter_dimension=0, tiled=True)  72.9 us
    reduce_scatter x1, waiting for transfers between devices, on_device(): lax.psum_scatter(fc_grad, 'dp', scatter_dimension=0, tiled=True)  69.1 us
    unnamed x2, blocking collectives  60.4 us
    pallas_call x1, Pallas kernels, attend_back(): pl.pallas_call(functools.partial(backward_kernel, heads), grid=(heads,),...  44.8 us
    reduce_scatter x1, waiting for transfers between devices, on_device(): lax.psum_scatter(times_trans(part, fc_full).astype(jnp.bfloat16), 'tensor...  43 us
    reduce_scatter x1, waiting for transfers between devices, on_device(): lax.psum_scatter(jnp.dot(part, out_full, preferred_element_type=jnp.float...  40.7 us
    all_gather x1, blocking collectives, on_device(): lax.all_gather(pieces[0], 'dp', axis=0, tiled=True)  35.5 us
  transfers between devices with their start and end apart: 14, of which 10 were waited for; matrix products, arithmetic and copies ran while one was open for 9% of the time, Pallas kernels for 6%

profile of v1, /device:TPU:0, one launch (start us, length us, event | category | flops | bytes accessed | tf_op | source)
XLA Modules:
  0.0 795.8 jit_solution(10467538680515351334)
XLA Ops:
  8.1 1.3 fusion.34
  10.1 0.8 dynamic-update-slice.1
  10.9 0.8 dynamic-update-slice.2
  11.8 0.8 dynamic-update-slice.3
  12.6 0.8 dynamic-update-slice
  13.4 23.4 %all-reduce.10 = (bf16[768]{0:T(1024)(128)(2,1)S(1)}, bf16[768]{0:T(1024)(128)(2,1)S(1)}, bf16[768]{0:T(1024)(128)(2,1)S(1)}, bf16[768]{0:T(1024)(128)(2,1)S(1)}) all-reduce(bf16[768]{0:T(1024)(128)(2,1)S(1)} %dynamic-update-slice.3, bf16[768]{0:T(1024)(128)(2,1)S(1)} %dynamic-update-slice.2, ...), channel_id=1, replica_groups=mesh['dp'=8,'tensor'=4] {'dp'}, use_global_device_ids=true, to_apply=%add.3 | all-reduce | flops 3072 | bytes 12288
  36.8 1.4 convert_reduce_fusion.2
  38.2 1.7 fusion.23
  39.9 1.4 fusion.18
  41.4 0.1 copy.37
  41.5 0.1 copy.34
  41.6 35.5 %all_gather.39 = bf16[768,3,192]{2,1,0:T(4,128)(2,1)S(1)} all-gather(bf16[96,3,192]{2,1,0:T(4,128)(2,1)S(1)} %copy.34), channel_id=1, replica_groups=mesh['dp'=8,'tensor'=4] {'dp'}, dimensions={0}, use_global_device_ids=true | all-gather | bytes 995328 | tf_op jit(solution)/shard_map/all_gather | solution.py:279
  77.2 2.0 copy.35
  79.2 33.7 %all_gather.40 = bf16[192,768]{0,1:T(8,128)(2,1)} all-gather(bf16[192,96]{0,1:T(8,128)(2,1)S(1)} %copy.37), channel_id=1, replica_groups=mesh['dp'=8,'tensor'=4] {'dp'}, dimensions={1}, use_global_device_ids=true | all-gather | bytes 331776 | tf_op jit(solution)/shard_map/all_gather | solution.py:280
  112.9 5.6 convolution_convert_fusion.4.qkv_ref
  118.5 34.4 %attend.1 = (bf16[2560,192]{1,0:T(8,128)(2,1)S(1)}, f32[3,1,2560]{2,1,0:T(1,128)S(1)}) custom-call(s32[1,8]{1,0:T(1,128)S(1)} %copy-done.5, bf16[2560,576]{1,0:T(8,128)(2,1)S(1)} %convolution_convert_fusion.4.qkv_ref), custom_call_target="tpu_custom_call" | custom-call | tf_op jit(solution)/shard_map/attend/pallas_call | solution.py:133
  152.9 1.0 copy-done.1
  153.9 3.1 convolution_convert_fusion.2
  157.1 0.5 all-gather.13.cloned.1.call-update
  157.7 0.5 all-gather.15.cloned.1.call-update
  158.3 0.5 all-gather.11.cloned.1.call-update
  158.9 40.7 %reduce-scatter.11.cloned.1.call-done = bf16[640,768]{1,0:T(8,128)(2,1)} async-done(((bf16[2560,768]{1,0:T(8,128)(2,1)}), bf16[640,768]{1,0:T(8,128)(2,1)}) %reduce-scatter.11.cloned.1.call-update) | async-done | bytes 983056 | tf_op jit(solution)/shard_map/reduce_scatter | solution.py:303
  199.6 1.6 fusion.31
  201.2 0.5 multiply_reduce_fusion
  201.7 1.5 add_convert_fusion.1
  203.2 0.2 reduce-scatter.15.cloned.1.call-start
  203.4 29.8 %all-gather.15.cloned.1.call-done = bf16[2560,768]{1,0:T(8,128)(2,1)} async-done(((bf16[640,768]{1,0:T(8,128)(2,1)}), bf16[2560,768]{1,0:T(8,128)(2,1)}) %all-gather.15.cloned.1.call-update) | async-done | bytes 3932176 | tf_op jit(solution)/shard_map/all_gather | solution.py:323
  233.2 8.8 %fusion.35 = f32[2560,768]{1,0:T(8,128)} fusion(bf16[2560,768]{1,0:T(8,128)(2,1)} %all-gather.15.cloned.1.call-done, bf16[768,768]{0,1:T(8,128)(2,1)} %all-gather.13.cloned.1.call-done), kind=kOutput, calls=%fused_computation.66 | convolution fusion | flops 3019898880 | bytes 12976128 | tf_op jit(solution)/shard_map/dot_general | solution.py:267
  242.0 34.7 %all-gather.11.cloned.1.call-done = bf16[768,768]{1,0:T(8,128)(2,1)} async-done(((bf16[96,768]{1,0:T(8,128)(2,1)}), bf16[768,768]{1,0:T(8,128)(2,1)}) %all-gather.11.cloned.1.call-update) | async-done | bytes 1179664 | tf_op jit(solution)/shard_map/all_gather | solution.py:281
  276.7 33.4 %all-gather.9.cloned.1.call-done = bf16[2560,768]{1,0:T(8,128)(2,1)} async-done(((bf16[640,768]{1,0:T(8,128)(2,1)}), bf16[2560,768]{1,0:T(8,128)(2,1)}) %all-gather.9.cloned.1.call-update) | async-done | bytes 3932176 | tf_op jit(solution)/shard_map/all_gather | solution.py:311
  310.1 12.1 %fusion.6 = (bf16[2560,768]{1,0:T(8,128)(2,1)S(1)}, f32[2560,768]{1,0:T(8,128)}) fusion(f32[2560,768]{1,0:T(8,128)} %fusion.35, bf16[2560,768]{1,0:T(8,128)(2,1)} %all-gather.9.cloned.1.call-done, bf16[768,768]{1,0:T(8,128)(2,1)} %all-gather.11.cloned.1.call-done), kind=kOutput, calls=%fused_computation.8 | convolution fusion | flops 3059220480 | bytes 24772608 | tf_op jit(solution)/shard_map/dot_general | solution.py:312
  322.3 1.9 copy-done.20
  324.2 4.8 convolution_convert_fusion
  329.1 43.0 %reduce-scatter.15.cloned.1.call-done = bf16[640,768]{1,0:T(8,128)(2,1)} async-done(((bf16[2560,768]{1,0:T(8,128)(2,1)}), bf16[640,768]{1,0:T(8,128)(2,1)}) %reduce-scatter.15.cloned.1.call-update) | async-done | bytes 983056 | tf_op jit(solution)/shard_map/reduce_scatter | solution.py:329
  372.1 2.4 fusion.29
  374.5 3.2 fusion.32
  377.8 32.9 %all-gather.17.cloned.1.call-done = bf16[2560,768]{1,0:T(8,128)(2,1)} async-done(((bf16[640,768]{1,0:T(8,128)(2,1)}), bf16[2560,768]{1,0:T(8,128)(2,1)}) %all-gather.17.cloned.1.call-update) | async-done | bytes 3932176 | tf_op jit(solution)/shard_map/all_gather | solution.py:336
  410.7 4.7 convolution_bitcast_fusion
  415.4 0.3 reduce-scatter.17.cloned.1.call-start
  415.7 4.5 convolution_convert_fusion.5
  420.2 1.5 copy.38.dmix_ref
  421.7 44.8 %attend_back.1 = bf16[2560,576]{1,0:T(8,128)(2,1)S(1)} custom-call(s32[1,8]{1,0:T(1,128)S(1)} %copy-done.5, bf16[2560,576]{1,0:T(8,128)(2,1)} %copy-done, bf16[2560,192]{1,0:T(8,128)(2,1)S(1)} %copy-done.2, bf16[2560,192]{1,0:T(8,128)(2,1)S(1)} %copy.38.dmix_ref, f32[3,1,2560]{2,1,0:T(1,128)S(1)} %get-tuple-element.13.lse_ref), custom_call_target="tpu_custom_call" | custom-call | tf_op jit(solution)/shard_map/attend_back/pallas_call | solution.py:221
  466.6 1.7 copy-done.3
  468.2 4.7 convolution_convert_fusion.3
  473.0 0.4 reduce-scatter.13.cloned.1.call-start
  473.5 0.8 copy-done.18
  474.2 10.0 %convolution_convert_fusion.1 = bf16[2560,768]{1,0:T(8,128)(2,1)} fusion(bf16[768,768]{0,1:T(8,128)(2,1)S(1)} %copy-done.18, f32[2560,768]{1,0:T(8,128)} %get-tuple-element.39), kind=kOutput, calls=%fused_computation.11 | convolution fusion | flops 3039559680 | bytes 12976128 | tf_op jit(solution)/shard_map/dot_general | solution.py:317
  484.4 8.9 %fusion.37 = f32[768,768]{1,0:T(8,128)} fusion(bf16[2560,768]{1,0:T(8,128)(2,1)} %all-gather.9.cloned.1.call-done, bf16[2560,768]{1,0:T(8,128)(2,1)} %copy-done.20), kind=kOutput, calls=%fused_computation.68 | convolution fusion | flops 3019898880 | bytes 10223616 | tf_op jit(solution)/shard_map/dot_general | solution.py:261
  493.4 9.8 %fusion.33 = f32[768,768]{0,1:T(8,128)} fusion(bf16[2560,768]{1,0:T(8,128)(2,1)} %all-gather.15.cloned.1.call-done, f32[2560,768]{1,0:T(8,128)} %get-tuple-element.39), kind=kOutput, calls=%fused_computation.64 | convolution fusion | flops 3037593600 | bytes 14155776 | tf_op jit(solution)/shard_map/dot_general | solution.py:261
  503.1 0.2 reduce-scatter.19.cloned.1.call-start
  503.4 6.0 fusion.36
  509.3 2.9 copy.39
  513.1 1.7 copy.42
  514.9 8.2 %reduce-scatter.17.cloned.1.call-done = bf16[640,768]{1,0:T(8,128)(2,1)} async-done(((bf16[2560,768]{1,0:T(8,128)(2,1)}), bf16[640,768]{1,0:T(8,128)(2,1)}) %reduce-scatter.17.cloned.1.call-update) | async-done | bytes 983056 | tf_op jit(solution)/shard_map/reduce_scatter | solution.py:342
  523.0 2.2 fusion.30
  525.2 37.1 %all-reduce.8 = (f32[768]{0:T(1024)S(1)}, f32[768]{0:T(1024)S(1)}, f32[768]{0:T(1024)S(1)}, f32[768]{0:T(1024)S(1)}) all-reduce(f32[768]{0:T(1024)S(1)} %get-tuple-element.16, f32[768]{0:T(1024)S(1)} %get-tuple-element.21, f32[768]{0:T(1024)S(1)} %get-tuple-element.14, ...), channel_id=10, replica_groups=mesh['dp'=8,'tensor'=4] {'dp'}, use_global_device_ids=true, to_apply=%region_17.0.clone | all-reduce | flops 3072 | bytes 24576
  562.3 0.1 dynamic-slice.5
  562.4 0.1 dynamic-slice.7
  562.5 0.1 dynamic-slice.9
  562.6 6.4 all-reduce.9
  569.0 4.1 fusion.22
  573.2 69.1 %reduce-scatter.21.cloned.1.call-done = f32[96,768]{1,0:T(8,128)} async-done(((f32[768,768]{1,0:T(8,128)}), f32[96,768]{1,0:T(8,128)}) %reduce-scatter.21.cloned.1.call-update) | async-done | bytes 294928 | tf_op jit(solution)/shard_map/reduce_scatter | solution.py:351
  642.3 73.1 %reduce-scatter.23.cloned.1.call-done = f32[768,96]{0,1:T(8,128)} async-done(((f32[768,768]{0,1:T(8,128)}), f32[768,96]{0,1:T(8,128)}) %reduce-scatter.23.cloned.1.call-update) | async-done | bytes 294928 | tf_op jit(solution)/shard_map/reduce_scatter | solution.py:352
  715.4 72.9 %reduce-scatter.19.cloned.1.call-done = f32[96,3,192]{2,0,1:T(8,128)} async-done(((f32[768,3,192]{2,0,1:T(8,128)}), f32[96,3,192]{2,0,1:T(8,128)}) %reduce-scatter.19.cloned.1.call-update) | async-done | bytes 221200 | tf_op jit(solution)/shard_map/reduce_scatter | solution.py:349
  (79 shorter events, 0.9 us)
Async XLA Ops:
  8.0 31.9 %copy-start.6 = (bf16[640,768]{1,0:T(8,128)(2,1)S(1)}, bf16[640,768]{1,0:T(8,128)(2,1)}, u32[]{:S(2)}) copy-start(bf16[640,768]{1,0:T(8,128)(2,1)} %param.11) | copy-start | bytes 2949124
  8.0 104.8 %all-gather.7.cloned.1.call-start = ((), (), s32[]{:S(2)}) async-start(), calls=%async_computation.8 | async-start | bytes 4915200 | tf_op jit(solution)/shard_map/all_gather | solution.py:299
  38.2 3.1 copy-start.17
  38.2 3.2 copy-start.16
  41.3 158.2 %reduce-scatter.11.cloned.1.call-start = ((), (), s32[]{:S(2)}) async-start(), calls=%async_computation.9 | async-start | bytes 4915200 | tf_op jit(solution)/shard_map/reduce_scatter | solution.py:303
  112.9 5.6 copy-start.5
  118.5 38.5 %copy-start = (bf16[2560,576]{1,0:T(8,128)(2,1)}, bf16[2560,576]{1,0:T(8,128)(2,1)S(1)}, u32[]{:S(2)}) copy-start(bf16[2560,576]{1,0:T(8,128)(2,1)S(1)} %convolution_convert_fusion.4.qkv_ref) | copy-start | bytes 8847364
  118.5 35.4 %copy-start.13 = (bf16[192,768]{0,1:T(8,128)(2,1)S(1)}, bf16[192,768]{0,1:T(8,128)(2,1)}, u32[]{:S(2)}) copy-start(bf16[192,768]{0,1:T(8,128)(2,1)} %all_gather.40) | copy-start | bytes 884740
  152.9 1.1 copy-start.1
  157.0 42.5 %copy-start.7 = (bf16[640,768]{1,0:T(8,128)(2,1)S(1)}, bf16[640,768]{1,0:T(8,128)(2,1)}, u32[]{:S(2)}) copy-start(bf16[640,768]{1,0:T(8,128)(2,1)} %param.11) | copy-start | bytes 2949124
  157.1 46.4 %all-gather.13.cloned.1.call-start = ((), (), s32[]{:S(2)}) async-start(), calls=%async_computation.12 | async-start | bytes 1327104 | tf_op jit(solution)/shard_map/all_gather | solution.py:282
  157.6 75.6 %all-gather.15.cloned.1.call-start = ((), (), s32[]{:S(2)}) async-start(), calls=%async_computation.14 | async-start | bytes 4915200 | tf_op jit(solution)/shard_map/all_gather | solution.py:323
  158.2 118.5 %all-gather.11.cloned.1.call-start = ((), (), s32[]{:S(2)}) async-start(), calls=%async_computation.11 | async-start | bytes 1327104 | tf_op jit(solution)/shard_map/all_gather | solution.py:281
  158.8 151.3 %all-gather.9.cloned.1.call-start = ((), (), s32[]{:S(2)}) async-start(), calls=%async_computation.10 | async-start | bytes 4915200 | tf_op jit(solution)/shard_map/all_gather | solution.py:311
  199.6 1.6 copy-start.9
  203.2 168.9 %reduce-scatter.15.cloned.1.call-start = ((), (), s32[]{:S(2)}) async-start(), calls=%async_computation.15 | async-start | bytes 4915200 | tf_op jit(solution)/shard_map/reduce_scatter | solution.py:329
  276.7 47.5 %copy-start.19 = (bf16[768,768]{1,0:T(8,128)(2,1)S(1)}, bf16[768,768]{1,0:T(8,128)(2,1)}, u32[]{:S(2)}) copy-start(bf16[768,768]{1,0:T(8,128)(2,1)} %all-gather.11.cloned.1.call-done) | copy-start | bytes 3538948
  322.3 1.9 copy-start.20
  329.1 81.7 %all-gather.17.cloned.1.call-start = ((), (), s32[]{:S(2)}) async-start(), calls=%async_computation.16 | async-start | bytes 4915200 | tf_op jit(solution)/shard_map/all_gather | solution.py:336
  372.1 2.4 copy-start.12
  374.5 36.2 %copy-start.2 = (bf16[2560,192]{1,0:T(8,128)(2,1)S(1)}, bf16[2560,192]{1,0:T(8,128)(2,1)}, u32[]{:S(2)}) copy-start(bf16[2560,192]{1,0:T(8,128)(2,1)} %copy-done.1) | copy-start | bytes 2949124
  377.8 37.9 %copy-start.14 = (bf16[192,768]{0,1:T(8,128)(2,1)S(1)}, bf16[192,768]{0,1:T(8,128)(2,1)}, u32[]{:S(2)}) copy-start(bf16[192,768]{0,1:T(8,128)(2,1)} %all_gather.40) | copy-start | bytes 884740
  377.8 135.4 %reduce-scatter.25.cloned.1.call-start = ((), (), s32[]{:S(2)}) async-start(), calls=%async_computation.21 | async-start | bytes 884736
  415.4 107.6 %reduce-scatter.17.cloned.1.call-start = ((), (), s32[]{:S(2)}) async-start(), calls=%async_computation.17 | async-start | bytes 4915200 | tf_op jit(solution)/shard_map/reduce_scatter | solution.py:342
  421.7 46.5 %copy-start.15 = (bf16[768,3,192]{0,2,1:T(8,128)(2,1)S(1)}, bf16[768,3,192]{0,2,1:T(8,128)(2,1)}, u32[]{:S(2)}) copy-start(bf16[768,3,192]{0,2,1:T(8,128)(2,1)} %copy.35) | copy-start | bytes 2654212
  466.6 1.7 copy-start.3
  473.0 1.3 copy-start.18
  473.0 96.0 %reduce-scatter.13.cloned.1.call-start = ((), (), s32[]{:S(2)}) async-start(), calls=%async_computation.13 | async-start | bytes 4915200 | tf_op jit(solution)/shard_map/reduce_scatter | solution.py:316
  484.3 158.0 %reduce-scatter.21.cloned.1.call-start = ((), (), s32[]{:S(2)}) async-start(), calls=%async_computation.19 | async-start | bytes 2654208 | tf_op jit(solution)/shard_map/reduce_scatter | solution.py:351
  493.3 222.1 %reduce-scatter.23.cloned.1.call-start = ((), (), s32[]{:S(2)}) async-start(), calls=%async_computation.20 | async-start | bytes 2654208 | tf_op jit(solution)/shard_map/reduce_scatter | solution.py:352
  493.3 10.0 %copy-start.4 = (bf16[2560,576]{1,0:T(8,128)(2,1)S(1)}, bf16[2560,576]{1,0:T(8,128)(2,1)}, u32[]{:S(2)}) copy-start(bf16[2560,576]{1,0:T(8,128)(2,1)} %copy-done.3) | copy-start | bytes 8847364
  503.1 285.1 %reduce-scatter.19.cloned.1.call-start = ((), (), s32[]{:S(2)}) async-start(), calls=%async_computation.18 | async-start | bytes 2654208 | tf_op jit(solution)/shard_map/reduce_scatter | solution.py:349
  512.3 10.8 %copy-start.8 = (bf16[640,768]{1,0:T(8,128)(2,1)S(1)}, bf16[640,768]{1,0:T(8,128)(2,1)}, u32[]{:S(2)}) copy-start(bf16[640,768]{1,0:T(8,128)(2,1)} %param.11) | copy-start | bytes 2949124
  512.3 56.8 %copy-start.10 = (bf16[640,768]{1,0:T(8,128)(2,1)S(1)}, bf16[640,768]{1,0:T(8,128)(2,1)}, u32[]{:S(2)}) copy-start(bf16[640,768]{1,0:T(8,128)(2,1)} %reduce-scatter.11.cloned.1.call-done) | copy-start | bytes 2949124
  512.3 56.8 %copy-start.11 = (bf16[640,768]{1,0:T(8,128)(2,1)S(1)}, bf16[640,768]{1,0:T(8,128)(2,1)}, u32[]{:S(2)}) copy-start(bf16[640,768]{1,0:T(8,128)(2,1)} %param.12) | copy-start | bytes 2949124
Sparse Core Ops, SparseCore 0:
  41.4 30.2 all-gather.6
  157.2 42.3 reduce-scatter.10
  329.2 42.8 reduce-scatter.14
Sparse Core Ops, SparseCore 1:
  159.7 40.8 all-gather.12
  202.0 31.2 all-gather.14
  235.3 41.4 all-gather.10
  278.9 31.2 all-gather.8
  377.8 32.8 all-gather.16
  415.5 63.2 reduce-scatter.24
  481.2 41.8 reduce-scatter.16
  525.4 42.8 reduce-scatter.12
  572.2 70.0 reduce-scatter.20
  646.4 68.9 reduce-scatter.22
  719.3 68.9 reduce-scatter.18

commit v2 on v1

--- a/solution.py
+++ b/solution.py
@@ -238,6 +238,250 @@
     )(lengths, qkv, mixed, dmix, lse)
 
 
+def around(axis_size):
+    spot = lax.axis_index("tensor")
+    return spot, spot + 1 - 2 * (spot % 2), (spot + 2) % 4, 3 - spot
+
+
+def greet(peers):
+    barrier = pltpu.get_barrier_semaphore()
+    for peer in peers:
+        pl.semaphore_signal(barrier, inc=1, device_id=peer, device_id_type=pl.DeviceIdType.MESH)
+    pl.semaphore_wait(barrier, len(peers))
+
+
+def push(source, target, sends, recvs, slot, peer):
+    copy = pltpu.make_async_remote_copy(
+        src_ref=source, dst_ref=target, send_sem=sends.at[slot], recv_sem=recvs.at[slot],
+        device_id=peer, device_id_type=pl.DeviceIdType.MESH,
+    )
+    copy.start()
+    return copy
+
+
+def span(start, count):
+    return pl.ds(pl.multiple_of(start, 16), count)
+
+
+def pieces_of(rows):
+    return 4 if rows % 64 == 0 else 1
+
+
+def gather_rows(mine, every, sends, recvs, ready):
+    size = mine.shape[0]
+    spot, partner, cross, diag = around(4)
+    pieces = pieces_of(size)
+    step = size // pieces
+    far, passed = [], []
+    for k in range(pieces):
+        far.append(push(mine.at[pl.ds(k * step, step)], every.at[span(spot * size + k * step, step)],
+                        sends, recvs, k, {"tensor": cross}))
+    near = push(mine, every.at[span(spot * size, size)], sends, recvs, pieces, {"tensor": partner})
+    every[span(spot * size, size), :] = mine[...]
+    ready(spot * size, size)
+    near.wait_recv()
+    ready(partner * size, size)
+    for k in range(pieces):
+        far[k].wait_recv()
+        block = every.at[span(cross * size + k * step, step)]
+        passed.append(push(block, block, sends, recvs, pieces + 1 + k, {"tensor": partner}))
+        ready(cross * size + k * step, step)
+        if k > 0:
+            passed[k - 1].wait_recv()
+            ready(diag * size + (k - 1) * step, step)
+    passed[-1].wait_recv()
+    ready(diag * size + (pieces - 1) * step, step)
+    for copy in far + [near] + passed:
+        copy.wait_send()
+
+
+def gather_kernel(mine, weight, every, product, sends, recvs):
+    spot, partner, cross, diag = around(4)
+    greet([{"tensor": partner}, {"tensor": cross}])
+
+    def ready(start, count):
+        at = span(start, count)
+        product[at, :] = nn(every[at, :], weight[...]).astype(product.dtype)
+
+    gather_rows(mine, every, sends, recvs, ready)
+
+
+def vmem():
+    return pl.BlockSpec(memory_space=pltpu.VMEM)
+
+
+def remote_params(ident):
+    return pltpu.CompilerParams(collective_id=ident, has_side_effects=True, vmem_limit_bytes=60 << 20)
+
+
+def gather_times(mine, weight, kind, ident):
+    size, width = mine.shape
+    count = 2 * pieces_of(size) + 1
+    return pl.pallas_call(
+        gather_kernel,
+        in_specs=[vmem(), vmem()],
+        out_specs=[vmem(), vmem()],
+        out_shape=[
+            jax.ShapeDtypeStruct((4 * size, width), mine.dtype),
+            jax.ShapeDtypeStruct((4 * size, weight.shape[1]), kind),
+        ],
+        scratch_shapes=[pltpu.SemaphoreType.DMA((count,)), pltpu.SemaphoreType.DMA((count,))],
+        compiler_params=remote_params(ident),
+        name=f"gather_times_{ident}",
+    )(mine, weight)
+
+
+def scatter_kernel(left, right, total, out_d, got_a, out_c, got_c, out_b, got_b, sends, recvs):
+    size = total.shape[0]
+    spot, partner, cross, diag = around(4)
+    pieces = pieces_of(size)
+    step = size // pieces
+    greet([{"tensor": partner}, {"tensor": cross}])
+
+    def part(block, k=0, count=size):
+        return nt(left[span(block * size + k * step, count), :], right[...])
+
+    first, second = [], []
+    for k in range(pieces):
+        at = pl.ds(k * step, step)
+        out_d[at, :] = part(diag, k, step).astype(jnp.bfloat16)
+        first.append(push(out_d.at[at], got_a.at[at], sends, recvs, k, {"tensor": partner}))
+    for k in range(pieces):
+        at = pl.ds(k * step, step)
+        term = part(cross, k, step)
+        first[k].wait_recv()
+        out_c[at, :] = (term + got_a[at, :].astype(jnp.float32)).astype(jnp.bfloat16)
+        second.append(push(out_c.at[at], got_c.at[at], sends, recvs, pieces + k, {"tensor": cross}))
+    out_b[...] = part(partner).astype(jnp.bfloat16)
+    third = push(out_b, got_b, sends, recvs, 2 * pieces, {"tensor": partner})
+    total[...] = part(spot)
+    third.wait_recv()
+    total[...] = total[...] + got_b[...].astype(jnp.float32)
+    for k in range(pieces):
+        at = pl.ds(k * step, step)
+        second[k].wait_recv()
+        total[at, :] = total[at, :] + got_c[at, :].astype(jnp.float32)
+    for copy in first + second + [third]:
+        copy.wait_send()
+
+
+def scatter_times(left, right, ident):
+    size, width = left.shape[0] // 4, right.shape[0]
+    count = 2 * pieces_of(size) + 1
+    return pl.pallas_call(
+        scatter_kernel,
+        in_specs=[vmem(), vmem()],
+        out_specs=vmem(),
+        out_shape=jax.ShapeDtypeStruct((size, width), jnp.float32),
+        scratch_shapes=[pltpu.VMEM((size, width), jnp.bfloat16)] * 6
+        + [pltpu.SemaphoreType.DMA((count,)), pltpu.SemaphoreType.DMA((count,))],
+        compiler_params=remote_params(ident),
+        name=f"scatter_times_{ident}",
+    )(left, right)
+
+
+def opening_kernel(
+    columns, tokens, small, shard, every, product, weights, gains, got_small, mine, sends, recvs, dp_sends, dp_recvs
+):
+    count = got_small.shape[0]
+    depth = shard.shape[0]
+    place = lax.axis_index("dp")
+    spot, partner, cross, diag = around(4)
+    others = [(place + i) % count for i in range(1, count)]
+    greet([{"dp": other} for other in others] + [{"tensor": partner}, {"tensor": cross}])
+    little, large = [], []
+    for i, other in enumerate(others):
+        little.append(push(small, got_small.at[place], dp_sends, dp_recvs, i, {"dp": other}))
+    for i, other in enumerate(others):
+        large.append(push(shard, weights.at[span(place * depth, depth)], dp_sends, dp_recvs, count - 1 + i, {"dp": other}))
+    got_small[place] = small[...]
+    weights[span(place * depth, depth), :] = shard[...]
+    for copy in little:
+        copy.wait_recv()
+    placed = functools.reduce(jnp.add, [got_small[i] for i in range(count)])
+    gains[...] = placed
+    values = tokens[...].astype(jnp.float32)
+    centred = values - jnp.mean(values, axis=-1, keepdims=True)
+    factor = lax.rsqrt(jnp.mean(centred * centred, axis=-1, keepdims=True) + 1e-05)
+    mine[...] = (centred * factor * placed[0:1, :] + placed[1:2, :]).astype(jnp.bfloat16)
+    landed = []
+
+    def ready(start, rows_count):
+        if not landed:
+            for copy in large:
+                copy.wait_recv()
+            landed.append(True)
+        at = span(start, rows_count)
+        product[at, :] = nn(every[at, :], weights[:, :columns]).astype(jnp.bfloat16)
+
+    gather_rows(mine, every, sends, recvs, ready)
+    for copy in little + large:
+        copy.wait_send()
+
+
+def opening(tokens, small, shard, columns, ident):
+    size, width = tokens.shape
+    count = 2 * pieces_of(size) + 1
+    dp = lax.axis_size("dp")
+    low = jnp.bfloat16
+    return pl.pallas_call(
+        functools.partial(opening_kernel, columns),
+        in_specs=[vmem()] * 3,
+        out_specs=[vmem()] * 4,
+        out_shape=[
+            jax.ShapeDtypeStruct((4 * size, width), low),
+            jax.ShapeDtypeStruct((4 * size, columns), low),
+            jax.ShapeDtypeStruct((dp * shard.shape[0], shard.shape[1]), low),
+            jax.ShapeDtypeStruct(small.shape, jnp.float32),
+        ],
+        scratch_shapes=[
+            pltpu.VMEM((dp,) + small.shape, jnp.float32),
+            pltpu.VMEM(tokens.shape, low),
+            pltpu.SemaphoreType.DMA((count,)), pltpu.SemaphoreType.DMA((count,)),
+            pltpu.SemaphoreType.DMA((2 * (dp - 1),)), pltpu.SemaphoreType.DMA((2 * (dp - 1),)),
+        ],
+        compiler_params=remote_params(ident),
+        name="opening",
+    )(tokens, small, shard)
+
+
+def vectors_kernel(parts, total, got, sends, recvs):
+    dp, tensor = parts.shape[0], got.shape[0] // parts.shape[0]
+    place, spot = lax.axis_index("dp"), lax.axis_index("tensor")
+    others = []
+    for i in range(dp):
+        for j in range(tensor):
+            if i or j:
+                others.append(((place + i) % dp, (spot + j) % tensor))
+    greet([{"dp": a, "tensor": b} for a, b in others])
+    here = place * tensor + spot
+    copies = []
+    for n, (a, b) in enumerate(others):
+        copies.append(push(parts.at[a], got.at[here], sends, recvs, n, {"dp": a, "tensor": b}))
+    got[here] = parts[place]
+    for copy in copies:
+        copy.wait_recv()
+    total[...] = functools.reduce(jnp.add, [got[n] for n in range(dp * tensor)])
+    for copy in copies:
+        copy.wait_send()
+
+
+def sum_vectors(parts, ident):
+    dp, tensor = lax.axis_size("dp"), lax.axis_size("tensor")
+    return pl.pallas_call(
+        vectors_kernel,
+        in_specs=[vmem()],
+        out_specs=vmem(),
+        out_shape=jax.ShapeDtypeStruct(parts.shape[1:], jnp.float32),
+        scratch_shapes=[
+            pltpu.VMEM((dp * tensor,) + parts.shape[1:], jnp.float32),
+            pltpu.SemaphoreType.DMA((dp * tensor - 1,)), pltpu.SemaphoreType.DMA((dp * tensor - 1,)),
+        ],
+        compiler_params=remote_params(ident),
+        name="sum_vectors",
+    )(parts)
+
+
 def normalize(values):
     mean = jnp.mean(values, axis=-1, keepdims=True)
     centred = values - mean
@@ -263,112 +507,92 @@
     )
 
 
-def times_trans(left, right):
-    return lax.dot_general(
-        left, right, (((1,), (1,)), ((), ())), preferred_element_type=jnp.float32
-    )
+def scatter_dp(grad):
+    return lax.psum_scatter(grad.astype(jnp.bfloat16), "dp", scatter_dimension=0, tiled=True).astype(jnp.float32)
+
+
+def spread(vectors, dp):
+    depth = vectors.shape[1]
+    owner = jnp.arange(dp * depth, dtype=jnp.int32) // depth
+    return jnp.where(owner[None, :] == lax.axis_index("dp"), jnp.tile(vectors, (1, dp)), 0.0)
 
 
 def on_device(
     tokens, cotangent, lengths, w_qkv, w_out, w_fc, w_proj, ln1_gain, ln1_bias, ln2_gain, ln2_bias
 ):
-    rows = tokens.shape[0]
-    group = rows * lax.axis_size("tensor")
-    pieces = (w_qkv, w_out, w_fc, w_proj, ln1_gain, ln1_bias, ln2_gain, ln2_bias)
-    qkv_full, out_full, fc_full, proj_full, gain1, bias1, gain2, bias2 = (
-        lax.all_gather(pieces[0], "dp", axis=0, tiled=True),
-        lax.all_gather(pieces[1], "dp", axis=1, tiled=True),
-        lax.all_gather(pieces[2], "dp", axis=0, tiled=True),
-        lax.all_gather(pieces[3], "dp", axis=1, tiled=True),
-        lax.all_gather(pieces[4], "dp", axis=0, tiled=True),
-        lax.all_gather(pieces[5], "dp", axis=0, tiled=True),
-        lax.all_gather(pieces[6], "dp", axis=0, tiled=True),
-        lax.all_gather(pieces[7], "dp", axis=0, tiled=True),
+    dp = lax.axis_size("dp")
+    low = jnp.bfloat16
+    depth, _, local = w_qkv.shape
+    width = depth * dp
+    heads = local // HEAD
+    small_dp = dp <= 8 and depth % 16 == 0
+    columns = 3 * local
+    inputs = tokens.astype(jnp.float32)
+    vectors = jnp.stack([ln1_gain, ln1_bias, ln2_gain, ln2_bias]).astype(jnp.float32)
+    shard = jnp.concatenate([w_qkv.reshape(depth, columns), w_out.T], axis=1)
+    if small_dp:
+        placed = jnp.concatenate([spread(vectors, dp), jnp.zeros((4, width), jnp.float32)])
+        all_norm1, projected, weights, gains = opening(tokens, placed, shard, columns, 0)
+    else:
+        gains = lax.psum(spread(vectors, dp), "dp")
+        weights = lax.all_gather(shard, "dp", axis=0, tiled=True)
+        lowered1 = (normalize(inputs)[0] * gains[0] + gains[1]).astype(low)
+        all_norm1, projected = gather_times(lowered1, weights[:, :columns], low, 0)
+    out_turned = weights[:, columns:]
+    w_fc, w_proj, cotangent_late, lengths, projected = lax.optimization_barrier(
+        (w_fc, w_proj, cotangent, lengths, projected)
     )
-    gain1 = gain1.astype(jnp.float32)
-    bias1 = bias1.astype(jnp.float32)
-    gain2 = gain2.astype(jnp.float32)
-    bias2 = bias2.astype(jnp.float32)
-    width = qkv_full.shape[0]
-    local = qkv_full.shape[2]
-    heads = local // HEAD
-    qkv_mat = qkv_full.reshape(width, 3 * local)
-    inputs = tokens.astype(jnp.float32)
-    normed1, factor1 = normalize(inputs)
-    lowered1 = (normed1 * gain1 + bias1).astype(jnp.bfloat16)
-    all_norm1 = lax.all_gather(lowered1, "tensor", axis=0, tiled=True)
-    projected = jnp.dot(all_norm1, qkv_mat, preferred_element_type=jnp.float32).astype(jnp.bfloat16)
+    fc_full = lax.all_gather(w_fc, "dp", axis=0, tiled=True)
+    proj_turned = lax.all_gather(w_proj.T, "dp", axis=0, tiled=True)
+    grad_all = lax.all_gather(cotangent_late, "tensor", axis=0, tiled=True)
+    gain1, gain2, bias2 = gains[0], gains[2], gains[3]
     mixed, sums = attend(projected, lengths, heads)
-    part = mixed
-    resid = inputs + lax.psum_scatter(
-        jnp.dot(part, out_full, preferred_element_type=jnp.float32).astype(jnp.bfloat16),
-        "tensor",
-        scatter_dimension=0,
-        tiled=True,
+    resid = inputs + scatter_times(mixed, out_turned, 1)
+    normed2, factor2 = normalize(resid)
+    lowered2 = (normed2 * gain2 + bias2).astype(low)
+    all_norm2, hidden_pre = gather_times(lowered2, fc_full, jnp.float32, 2)
+    hidden, gelu_pull = jax.vjp(gelu_tanh, hidden_pre)
+    hidden_low = hidden.astype(low)
+    mlp_rows = lax.psum_scatter(
+        nt(hidden_low, proj_turned).astype(low), "tensor", scatter_dimension=0, tiled=True
     ).astype(jnp.float32)
-    normed2, factor2 = normalize(resid)
-    lowered2 = (normed2 * gain2 + bias2).astype(jnp.bfloat16)
-    all_norm2 = lax.all_gather(lowered2, "tensor", axis=0, tiled=True)
-    hidden_pre = jnp.dot(all_norm2, fc_full, preferred_element_type=jnp.float32)
-    hidden, gelu_pull = jax.vjp(gelu_tanh, hidden_pre)
-    hidden_low = hidden.astype(jnp.bfloat16)
-    part = hidden_low
-    mlp_rows = lax.psum_scatter(
-        jnp.dot(part, proj_full, preferred_element_type=jnp.float32).astype(jnp.bfloat16),
-        "tensor",
-        scatter_dimension=0,
-        tiled=True,
-    ).astype(jnp.float32)
-    block_out = (resid + mlp_rows).astype(jnp.bfloat16)
-    grad_all = lax.all_gather(cotangent, "tensor", axis=0, tiled=True)
-    hidden_grad = times_trans(grad_all, proj_full)
-    proj_grad = inner_rows(hidden_low, grad_all)
-    pre_low = gelu_pull(hidden_grad)[0].astype(jnp.bfloat16)
+    block_out = (resid + mlp_rows).astype(low)
+    hidden_grad = nn(grad_all, proj_turned)
+    proj_grad = inner_rows(grad_all, hidden_low)
+    pre_low = gelu_pull(hidden_grad)[0].astype(low)
     fc_grad = inner_rows(all_norm2, pre_low)
-    part = pre_low
-    norm2_grad = lax.psum_scatter(
-        times_trans(part, fc_full).astype(jnp.bfloat16), "tensor", scatter_dimension=0, tiled=True
-    ).astype(jnp.float32)
+    norm2_grad = scatter_times(pre_low, fc_full, 3)
+    proj_sum = scatter_dp(proj_grad).T
+    fc_sum = scatter_dp(fc_grad)
     gain2_part = jnp.sum(norm2_grad * normed2, axis=0)
     bias2_part = jnp.sum(norm2_grad, axis=0)
     resid_grad = cotangent.astype(jnp.float32) + norm_back(norm2_grad, normed2, factor2, gain2)
-    resid_low = resid_grad.astype(jnp.bfloat16)
-    resid_all = lax.all_gather(resid_low, "tensor", axis=0, tiled=True)
-    out_grad = inner_rows(mixed, resid_all)
-    mixed_grad = times_trans(resid_all, out_full).astype(jnp.bfloat16)
+    resid_all, mixed_grad = gather_times(resid_grad.astype(low), out_turned, low, 4)
     qkv_grad_low = attend_back(projected, mixed, mixed_grad, sums, lengths, heads)
-    qkv_grad = inner_rows(all_norm1, qkv_grad_low).reshape(width, 3, local)
-    part = qkv_grad_low
-    norm1_grad = lax.psum_scatter(
-        times_trans(part, qkv_mat).astype(jnp.bfloat16), "tensor", scatter_dimension=0, tiled=True
-    ).astype(jnp.float32)
-    gain1_part = jnp.sum(norm1_grad * normed1, axis=0)
-    bias1_part = jnp.sum(norm1_grad, axis=0)
-    input_grad = (resid_grad + norm_back(norm1_grad, normed1, factor1, gain1)).astype(jnp.bfloat16)
-    qkv_sum, out_sum, fc_sum, proj_sum, gain1_share, bias1_share, gain2_share, bias2_share = (
-        lax.psum_scatter(qkv_grad, "dp", scatter_dimension=0, tiled=True),
-        lax.psum_scatter(out_grad, "dp", scatter_dimension=1, tiled=True),
-        lax.psum_scatter(fc_grad, "dp", scatter_dimension=0, tiled=True),
-        lax.psum_scatter(proj_grad, "dp", scatter_dimension=1, tiled=True),
-        lax.psum_scatter(gain1_part, "dp", scatter_dimension=0, tiled=True),
-        lax.psum_scatter(bias1_part, "dp", scatter_dimension=0, tiled=True),
-        lax.psum_scatter(gain2_part, "dp", scatter_dimension=0, tiled=True),
-        lax.psum_scatter(bias2_part, "dp", scatter_dimension=0, tiled=True),
+    last_grad = jnp.concatenate(
+        [inner_rows(all_norm1, qkv_grad_low).astype(low), inner_rows(resid_all, mixed).astype(low)], axis=1
     )
-    gain1_sum, bias1_sum, gain2_sum, bias2_sum = lax.psum(
-        (gain1_share, bias1_share, gain2_share, bias2_share), "tensor"
-    )
+    last_sum = scatter_dp(last_grad)
+    norm1_grad = scatter_times(qkv_grad_low, weights[:, :columns], 5)
+    normed1, factor1 = normalize(inputs)
+    input_grad = (resid_grad + norm_back(norm1_grad, normed1, factor1, gain1)).astype(low)
+    parts = jnp.stack([jnp.sum(norm1_grad * normed1, axis=0), jnp.sum(norm1_grad, axis=0), gain2_part, bias2_part])
+    if small_dp:
+        pieces = jnp.pad(parts.reshape(4, dp, depth).transpose(1, 0, 2), ((0, 0), (0, 4), (0, -depth % 128)))
+        shares = sum_vectors(pieces, 6)[:4, :depth]
+    else:
+        shares = lax.psum(lax.psum_scatter(parts, "dp", scatter_dimension=1, tiled=True), "tensor")
     return (
         block_out,
         input_grad,
-        qkv_sum,
-        out_sum,
+        last_sum[:, :columns].reshape(depth, 3, local),
+        last_sum[:, columns:].T,
         fc_sum,
         proj_sum,
-        gain1_sum,
-        bias1_sum,
-        gain2_sum,
-        bias2_sum,
+        shares[0],
+        shares[1],
+        shares[2],
+        shares[3],
     )
 
 

time: 799 us -> 468 us (0.59)
  waiting for transfers between devices: 440 us -> 65.2 us
  Pallas kernels: 79.2 us -> 296 us
  blocking collectives: 136 us -> 0 us
  matrix products: 83 us -> 39 us
    reduce_scatter x7 -> x3, waiting for transfers between devices: 307 us -> 34.8 us  [the longest x2 34.8 us: scatter_dp(): lax.psum_scatter(grad.astype(jnp.bfloat16), 'dp', scatter_dimension=0, ti...]
    pallas_call x0 -> x7, Pallas kernels: none -> 216 us  [the longest x3 107 us: scatter_times(): pl.pallas_call(scatter_kernel, in_specs=[vmem(), vmem()], out_specs=vmem(...]
    all_gather x6 -> x3, waiting for transfers between devices: 131 us -> 11.3 us  [the longest x1 11.2 us: on_device(): grad_all = lax.all_gather(cotangent_late, 'tensor', axis=0, tiled=True)]
    all_gather x2 -> x0, blocking collectives: 69.2 us -> none  [the longest x1 35.5 us: on_device(): lax.all_gather(pieces[0], 'dp', axis=0, tiled=True)]
    unnamed x2 -> x0, blocking collectives: 60.4 us -> none
    dot_general x8 -> x2, matrix products: 53.7 us -> 20.6 us  [the longest x1 10.4 us: nt(): lax.dot_general(left, right, (((1,), (1,)), ((), ())), preferred_element_...]
    unnamed x15 -> x8, waiting for transfers between devices: 1.79 us -> 19.1 us
    dot_general x3 -> x4, matrix products: 24.6 us -> 18.3 us  [inner_rows(): lax.dot_general(left, right, (((0,), (0,)), ((), ())), preferred_element_...]
  transfers between devices with their start and end apart: 14 -> 7, of which waited for: 10 -> 3; matrix products, arithmetic and copies ran while one was open for 9% -> 15% of each run, Pallas kernels for 6% -> 56%
where the time goes in v2:
time: 468 us; the launch traced here: 459 us
  Pallas kernels  296 us (63%)
  waiting for transfers between devices  65.2 us (14%)
  matrix products  39 us (8%)
  local copies, waits for them, and re-layouts  22.9 us (5%)
  other arithmetic  21.7 us (5%)
  between operations  14.7 us (3%)
    pallas_call x3, Pallas kernels, scatter_times(): pl.pallas_call(scatter_kernel, in_specs=[vmem(), vmem()], out_specs=vmem(...  107 us
    pallas_call x2, Pallas kernels, gather_times(): pl.pallas_call(gather_kernel, in_specs=[vmem(), vmem()], out_specs=[vmem(...  59.8 us
    pallas_call x1, Pallas kernels, attend_back(): pl.pallas_call(functools.partial(backward_kernel, heads), grid=(heads,),...  45.1 us
    pallas_call x1, Pallas kernels, opening(): pl.pallas_call(functools.partial(opening_kernel, columns), in_specs=[vmem...  39.5 us
    pallas_call x1, Pallas kernels, attend(): pl.pallas_call(functools.partial(forward_kernel, heads), grid=(heads,), i...  34.9 us
    reduce_scatter x2, waiting for transfers between devices, scatter_dp(): lax.psum_scatter(grad.astype(jnp.bfloat16), 'dp', scatter_dimension=0, ti...  34.8 us
    unnamed x8, waiting for transfers between devices  19.1 us
    dot_general x4, matrix products, inner_rows(): lax.dot_general(left, right, (((0,), (0,)), ((), ())), preferred_element_...  18.3 us
  transfers between devices with their start and end apart: 7, of which 3 were waited for; matrix products, arithmetic and copies ran while one was open for 15% of the time, Pallas kernels for 56%

profile of v2, /device:TPU:0, one launch (start us, length us, event | category | flops | bytes accessed | tf_op | source)
XLA Modules:
  0.0 459.5 jit_solution(1290102985763280051)
XLA Ops:
  7.2 0.0 all-gather.4.cloned.1.call-start
  7.2 0.7 maximum_convert_fusion
  8.0 0.1 tile.10
  8.1 0.9 copy.29
  8.9 1.1 copy.28
  10.0 0.1 copy.30
  10.2 0.6 concatenate.14.small
  10.8 0.7 pad_maximum_fusion.1.shard
  11.6 39.5 %opening.1 = (bf16[2560,768]{1,0:T(8,128)(2,1)}, bf16[2560,576]{1,0:T(8,128)(2,1)}, bf16[768,768]{1,0:T(8,128)(2,1)}, f32[8,768]{1,0:T(8,128)}) custom-call(bf16[640,768]{1,0:T(8,128)(2,1)} %tokens.1, f32[8,768]{1,0:T(8,128)} %concatenate.14.small, bf16[96,768]{1,0:T(8,128)(2,1)} %pad_maximum_fusion.1.shard), custom_call_target="tpu_custom_call" | custom-call | tf_op jit(solution)/shard_map/opening/pallas_call | solution.py:427
  51.1 0.0 all-gather.6.cloned.1.call-start
  51.2 0.7 all-gather.6.cloned.1.call-update
  51.9 0.7 all-gather.8.cloned.1.call-update
  52.6 0.0 reduce-scatter.7.cloned.1.call-start
  52.7 1.9 slice.38.right.weight
  54.6 1.9 copy-done.1
  56.5 34.9 %attend.1 = (bf16[2560,192]{1,0:T(8,128)(2,1)S(1)}, f32[3,1,2560]{2,1,0:T(1,128)S(1)}) custom-call(s32[1,8]{1,0:T(1,128)S(1)} %copy-done.5, bf16[2560,576]{1,0:T(8,128)(2,1)S(1)} %copy-done.1), custom_call_target="tpu_custom_call" | custom-call | tf_op jit(solution)/shard_map/attend/pallas_call | solution.py:133
  91.4 1.1 copy-done.2
  92.5 29.0 %scatter_times_1.1 = f32[640,768]{1,0:T(8,128)} custom-call(bf16[2560,192]{1,0:T(8,128)(2,1)} %copy-done.2, bf16[768,192]{1,0:T(8,128)(2,1)} %slice.38.right.weight), custom_call_target="tpu_custom_call" | custom-call | tf_op jit(solution)/shard_map/scatter_times_1/pallas_call | solution.py:371
  121.5 0.9 slice_reduce_fusion
  122.4 0.2 convert_reduce_fusion
  122.6 2.2 fusion.24
  124.9 0.4 multiply_reduce_fusion.2
  125.3 1.3 add_convert_fusion.1.mine
  126.6 31.4 %gather_times_2.1 = (bf16[2560,768]{1,0:T(8,128)(2,1)}, f32[2560,768]{1,0:T(8,128)}) custom-call(bf16[640,768]{1,0:T(8,128)(2,1)} %add_convert_fusion.1.mine, bf16[768,768]{1,0:T(8,128)(2,1)} %all-gather.4.cloned.1.call-done.weight.right), custom_call_target="tpu_custom_call" | custom-call | tf_op jit(solution)/shard_map/gather_times_2/pallas_call | solution.py:320
  158.0 10.4 %convolution_convert_fusion = bf16[2560,768]{1,0:T(8,128)(2,1)} fusion(bf16[768,768]{1,0:T(8,128)(2,1)} %all-gather.6.cloned.1.call-done, f32[2560,768]{1,0:T(8,128)} %get-tuple-element.32), kind=kOutput, calls=%fused_computation.10 | convolution fusion | flops 3039559680 | bytes 12976128 | tf_op jit(solution)/shard_map/dot_general | solution.py:18
  168.5 0.0 reduce-scatter.9.cloned.1.call-start
  168.5 11.2 %all-gather.8.cloned.1.call-done = bf16[2560,768]{1,0:T(8,128)(2,1)} async-done(((bf16[640,768]{1,0:T(8,128)(2,1)}), bf16[2560,768]{1,0:T(8,128)(2,1)}) %all-gather.8.cloned.1.call-update) | async-done | bytes 3932176 | tf_op jit(solution)/shard_map/all_gather | solution.py:547
  179.7 10.2 %fusion.6.left = bf16[2560,768]{1,0:T(8,128)(2,1)S(1)} fusion(f32[2560,768]{1,0:T(8,128)} %get-tuple-element.32, bf16[2560,768]{1,0:T(8,128)(2,1)} %all-gather.8.cloned.1.call-done, bf16[768,768]{1,0:T(8,128)(2,1)} %all-gather.6.cloned.1.call-done), kind=kOutput, calls=%fused_computation.8 | convolution fusion | flops 3059220480 | bytes 16908288 | tf_op jit(solution)/shard_map/dot_general | solution.py:22
  190.0 1.9 copy-done.9
  191.9 4.3 convolution_convert_fusion.2
  196.2 0.0 reduce-scatter.11.cloned.1.call-start
  196.2 10.4 %convolution_convert_fusion.1 = bf16[768,768]{1,0:T(8,128)(2,1)} fusion(bf16[2560,768]{1,0:T(8,128)(2,1)} %all-gather.8.cloned.1.call-done, f32[2560,768]{1,0:T(8,128)} %get-tuple-element.32), kind=kOutput, calls=%fused_computation.35 | convolution fusion | flops 3038183424 | bytes 12976128 | tf_op jit(solution)/shard_map/dot_general | solution.py:505
  206.6 0.0 reduce-scatter.13.cloned.1.call-start
  206.7 47.3 %scatter_times_3.1 = f32[640,768]{1,0:T(8,128)} custom-call(bf16[2560,768]{1,0:T(8,128)(2,1)} %copy-done.9, bf16[768,768]{1,0:T(8,128)(2,1)} %all-gather.4.cloned.1.call-done.weight.right), custom_call_target="tpu_custom_call" | custom-call | tf_op jit(solution)/shard_map/scatter_times_3/pallas_call | solution.py:371
  254.0 2.5 multiply_reduce_fusion
  256.6 4.3 fusion.23
  260.8 28.4 %gather_times_4.1 = (bf16[2560,768]{1,0:T(8,128)(2,1)}, bf16[2560,192]{1,0:T(8,128)(2,1)}) custom-call(bf16[640,768]{1,0:T(8,128)(2,1)} %get-tuple-element.81.mine, bf16[768,192]{1,0:T(8,128)(2,1)} %slice.38.right.weight), custom_call_target="tpu_custom_call" | custom-call | tf_op jit(solution)/shard_map/gather_times_4/pallas_call | solution.py:320
  289.3 1.3 copy-done.3
  290.6 1.3 copy-done.4
  291.9 45.1 %attend_back.1.left = bf16[2560,576]{1,0:T(8,128)(2,1)S(1)} custom-call(s32[1,8]{1,0:T(1,128)S(1)} %copy-done.5, bf16[2560,576]{1,0:T(8,128)(2,1)} %get-tuple-element.27.qkv_ref, bf16[2560,192]{1,0:T(8,128)(2,1)S(1)} %copy-done.3, bf16[2560,192]{1,0:T(8,128)(2,1)S(1)} %copy-done.4, f32[3,1,2560]{2,1,0:T(1,128)S(1)} %get-tuple-element.36.lse_ref), custom_call_target="tpu_custom_call" | custom-call | tf_op jit(solution)/shard_map/attend_back/pallas_call | solution.py:221
  337.1 1.0 convolution_convert_fusion.4
  338.1 0.7 copy-done
  338.8 1.6 copy-done.12
  340.4 2.7 convolution_convert_fusion.3
  343.1 0.1 pad_maximum_fusion
  343.2 1.5 copy.32
  344.7 1.0 slice.41.right
  345.7 0.1 stack.37
  345.8 0.1 stack.38
  345.9 1.6 convert_element_type.73
  347.5 34.8 %reduce-scatter.11.cloned.1.call-done = bf16[96,768]{1,0:T(8,128)(2,1)} async-done(((bf16[768,768]{1,0:T(8,128)(2,1)}), bf16[96,768]{1,0:T(8,128)(2,1)}) %reduce-scatter.11.cloned.1.call-update) | async-done | bytes 147472 | tf_op jit(solution)/shard_map/reduce_scatter | solution.py:511
  382.4 1.6 convert_bitcast_fusion
  384.0 30.5 %scatter_times_5.1 = f32[640,768]{1,0:T(8,128)} custom-call(bf16[2560,576]{1,0:T(8,128)(2,1)} %copy-done, bf16[768,576]{1,0:T(8,128)(2,1)} %slice.41.right), custom_call_target="tpu_custom_call" | custom-call | tf_op jit(solution)/shard_map/scatter_times_5/pallas_call | solution.py:371
  414.5 2.6 fusion.17
  417.2 0.1 stack.35
  417.3 0.1 stack.36
  417.4 0.6 pad.5.parts
  418.0 9.6 %sum_vectors.1 = f32[8,128]{1,0:T(8,128)} custom-call(f32[8,8,128]{2,1,0:T(8,128)} %pad.5.parts), custom_call_target="tpu_custom_call" | custom-call | tf_op jit(solution)/shard_map/sum_vectors/pallas_call | solution.py:471
  427.6 1.3 slice_bitcast_fusion.1
  429.0 3.2 fusion.16
  432.2 17.6 %reduce-scatter.13.cloned.1.call-done = bf16[96,768]{1,0:T(8,128)(2,1)} async-done(((bf16[768,768]{1,0:T(8,128)(2,1)}), bf16[96,768]{1,0:T(8,128)(2,1)}) %reduce-scatter.13.cloned.1.call-update) | async-done | bytes 147472
  449.8 1.1 copy.33
  450.9 0.9 copy.31
  451.8 0.6 slice_bitcast_fusion
  (46 shorter events, 0.4 us)
Async XLA Ops:
  7.2 119.4 %all-gather.4.cloned.1.call-start = ((), (), s32[]{:S(2)}) async-start(), calls=%async_computation.4 | async-start | bytes 1327104 | tf_op jit(solution)/shard_map/all_gather | solution.py:545
  10.0 44.6 %copy-start.5 = (s32[1,8]{1,0:T(1,128)S(1)}, s32[1,8]{1,0:T(1,128)}, u32[]{:S(2)}) copy-start(s32[1,8]{1,0:T(1,128)} %lengths_ref.1) | copy-start | bytes 100
  51.1 106.9 %all-gather.6.cloned.1.call-start = ((), (), s32[]{:S(2)}) async-start(), calls=%async_computation.5 | async-start | bytes 1327104 | tf_op jit(solution)/shard_map/all_gather | solution.py:546
  51.9 127.9 %all-gather.8.cloned.1.call-start = ((), (), s32[]{:S(2)}) async-start(), calls=%async_computation.7 | async-start | bytes 4915200 | tf_op jit(solution)/shard_map/all_gather | solution.py:547
  52.6 203.9 %reduce-scatter.7.cloned.1.call-start = ((), (), s32[]{:S(2)}) async-start(), calls=%async_computation.6 | async-start | bytes 4915200 | tf_op jit(solution)/shard_map/reduce_scatter | solution.py:556
  54.6 1.9 copy-start.1
  91.4 1.1 copy-start.2
  92.5 29.9 %copy-start.6 = (bf16[640,768]{1,0:T(8,128)(2,1)S(1)}, bf16[640,768]{1,0:T(8,128)(2,1)}, u32[]{:S(2)}) copy-start(bf16[640,768]{1,0:T(8,128)(2,1)} %tokens.1) | copy-start | bytes 2949124
  168.5 177.4 %reduce-scatter.9.cloned.1.call-start = ((), (), s32[]{:S(2)}) async-start(), calls=%async_computation.8 | async-start | bytes 1327104 | tf_op jit(solution)/shard_map/reduce_scatter | solution.py:511
  179.7 12.1 %copy-start.13 = (bf16[2560,768]{1,0:T(8,128)(2,1)S(1)}, bf16[2560,768]{1,0:T(8,128)(2,1)}, u32[]{:S(2)}) copy-start(bf16[2560,768]{1,0:T(8,128)(2,1)} %get-tuple-element.39) | copy-start | bytes 11796484
  190.0 1.9 copy-start.9
  196.2 186.2 %reduce-scatter.11.cloned.1.call-start = ((), (), s32[]{:S(2)}) async-start(), calls=%async_computation.9 | async-start | bytes 1327104 | tf_op jit(solution)/shard_map/reduce_scatter | solution.py:511
  206.6 243.2 %reduce-scatter.13.cloned.1.call-start = ((), (), s32[]{:S(2)}) async-start(), calls=%async_computation.10 | async-start | bytes 1327104
  253.9 2.6 copy-start.10
  289.3 1.3 copy-start.3
  290.6 1.3 copy-start.4
  291.9 45.2 %copy-start.14 = (bf16[2560,768]{1,0:T(8,128)(2,1)S(1)}, bf16[2560,768]{1,0:T(8,128)(2,1)}, u32[]{:S(2)}) copy-start(bf16[2560,768]{1,0:T(8,128)(2,1)} %get-tuple-element.38) | copy-start | bytes 11796484
  337.1 1.7 copy-start
  337.1 3.3 copy-start.12
  343.2 1.5 copy-start.11
  384.0 30.5 %copy-start.7 = (bf16[640,768]{1,0:T(8,128)(2,1)S(1)}, bf16[640,768]{1,0:T(8,128)(2,1)}, u32[]{:S(2)}) copy-start(bf16[640,768]{1,0:T(8,128)(2,1)} %tokens.1) | copy-start | bytes 2949124
  414.5 14.5 %copy-start.8 = (f32[640,768]{1,0:T(8,128)S(1)}, f32[640,768]{1,0:T(8,128)}, u32[]{:S(2)}) copy-start(f32[640,768]{1,0:T(8,128)} %scatter_times_5.1) | copy-start | bytes 5898244
Sparse Core Ops, SparseCore 0:
  51.3 53.4 all-gather.3
  106.9 39.7 all-gather.5
  148.3 31.4 all-gather.7
  182.1 66.0 reduce-scatter.6
  251.5 63.8 reduce-scatter.8
  318.6 63.6 reduce-scatter.10
  385.7 63.9 reduce-scatter.12

commit v3 on v2

--- a/solution.py
+++ b/solution.py
@@ -306,6 +306,54 @@
     gather_rows(mine, every, sends, recvs, ready)
 
 
+def exchange_out(grad, got, sends, recvs):
+    count, depth = got.shape[0], got.shape[1]
+    place = lax.axis_index("dp")
+    copies = []
+    for i in range(1, count):
+        other = (place + i) % count
+        copies.append(push(grad.at[span(other * depth, depth), :], got.at[place], sends, recvs, i - 1, {"dp": other}))
+    got[place] = grad[span(place * depth, depth), :]
+    return copies
+
+
+def exchange_in(copies, got, total):
+    for copy in copies:
+        copy.wait_recv()
+    total[...] = functools.reduce(jnp.add, [got[i].astype(jnp.float32) for i in range(got.shape[0])])
+    for copy in copies:
+        copy.wait_send()
+
+
+def spread_out(shard, every, count, sends, recvs):
+    depth = shard.shape[0]
+    place = lax.axis_index("dp")
+    copies = []
+    for i in range(1, count):
+        other = (place + i) % count
+        copies.append(push(shard, every.at[span(place * depth, depth), :], sends, recvs, i - 1, {"dp": other}))
+    every[span(place * depth, depth), :] = shard[...]
+    return copies
+
+
+def dp_peers(count):
+    place = lax.axis_index("dp")
+    return [{"dp": (place + i) % count} for i in range(1, count)]
+
+
+def gather_exchange_kernel(dp, mine, weight, grad, every, product, total, sends, recvs, got, dp_sends, dp_recvs):
+    spot, partner, cross, diag = around(4)
+    greet(dp_peers(dp) + [{"tensor": partner}, {"tensor": cross}])
+    copies = exchange_out(grad, got, dp_sends, dp_recvs)
+
+    def ready(start, count):
+        at = span(start, count)
+        product[at, :] = nn(every[at, :], weight[...]).astype(product.dtype)
+
+    gather_rows(mine, every, sends, recvs, ready)
+    exchange_in(copies, got, total)
+
+
 def vmem():
     return pl.BlockSpec(memory_space=pltpu.VMEM)
 
@@ -314,29 +362,74 @@
     return pltpu.CompilerParams(collective_id=ident, has_side_effects=True, vmem_limit_bytes=60 << 20)
 
 
-def gather_times(mine, weight, kind, ident):
+def side_room(dp, grad):
+    return [
+        pltpu.VMEM((dp, grad.shape[0] // dp, grad.shape[1]), grad.dtype),
+        pltpu.SemaphoreType.DMA((dp - 1,)), pltpu.SemaphoreType.DMA((dp - 1,)),
+    ]
+
+
+def side_shape(dp, grad):
+    return jax.ShapeDtypeStruct((grad.shape[0] // dp, grad.shape[1]), jnp.float32)
+
+
+def gather_times(mine, weight, kind, ident, grad=None):
     size, width = mine.shape
     count = 2 * pieces_of(size) + 1
+    dp = lax.axis_size("dp")
+    shapes = [
+        jax.ShapeDtypeStruct((4 * size, width), mine.dtype),
+        jax.ShapeDtypeStruct((4 * size, weight.shape[1]), kind),
+    ]
+    sems = [pltpu.SemaphoreType.DMA((count,)), pltpu.SemaphoreType.DMA((count,))]
+    if grad is None:
+        body, operands = gather_kernel, (mine, weight)
+    else:
+        body, operands = functools.partial(gather_exchange_kernel, dp), (mine, weight, grad)
+        shapes, sems = shapes + [side_shape(dp, grad)], sems + side_room(dp, grad)
     return pl.pallas_call(
-        gather_kernel,
-        in_specs=[vmem(), vmem()],
-        out_specs=[vmem(), vmem()],
-        out_shape=[
-            jax.ShapeDtypeStruct((4 * size, width), mine.dtype),
-            jax.ShapeDtypeStruct((4 * size, weight.shape[1]), kind),
-        ],
-        scratch_shapes=[pltpu.SemaphoreType.DMA((count,)), pltpu.SemaphoreType.DMA((count,))],
+        body,
+        in_specs=[vmem()] * len(operands),
+        out_specs=[vmem()] * len(shapes),
+        out_shape=shapes,
+        scratch_shapes=sems,
         compiler_params=remote_params(ident),
         name=f"gather_times_{ident}",
-    )(mine, weight)
-
-
-def scatter_kernel(left, right, total, out_d, got_a, out_c, got_c, out_b, got_b, sends, recvs):
+    )(*operands)
+
+
+def scatter_kernel(left, right, total, *room):
+    spot, partner, cross, diag = around(4)
+    greet([{"tensor": partner}, {"tensor": cross}])
+    scatter_rows(left, right, total, *room)
+
+
+def scatter_exchange_kernel(dp, left, right, grad, total, summed, *room):
+    got, dp_sends, dp_recvs = room[-3:]
+    spot, partner, cross, diag = around(4)
+    greet(dp_peers(dp) + [{"tensor": partner}, {"tensor": cross}])
+    copies = exchange_out(grad, got, dp_sends, dp_recvs)
+    scatter_rows(left, right, total, *room[:-3])
+    exchange_in(copies, got, summed)
+
+
+def scatter_spread_kernel(dp, left, right, shard, total, every, *room):
+    dp_sends, dp_recvs = room[-2:]
+    spot, partner, cross, diag = around(4)
+    greet(dp_peers(dp) + [{"tensor": partner}, {"tensor": cross}])
+    copies = spread_out(shard, every, dp, dp_sends, dp_recvs)
+    scatter_rows(left, right, total, *room[:-2])
+    for copy in copies:
+        copy.wait_recv()
+    for copy in copies:
+        copy.wait_send()
+
+
+def scatter_rows(left, right, total, out_d, got_a, out_c, got_c, out_b, got_b, sends, recvs):
     size = total.shape[0]
     spot, partner, cross, diag = around(4)
     pieces = pieces_of(size)
     step = size // pieces
-    greet([{"tensor": partner}, {"tensor": cross}])
 
     def part(block, k=0, count=size):
         return nt(left[span(block * size + k * step, count), :], right[...])
@@ -365,19 +458,30 @@
         copy.wait_send()
 
 
-def scatter_times(left, right, ident):
+def scatter_times(left, right, ident, grad=None, shard=None):
     size, width = left.shape[0] // 4, right.shape[0]
     count = 2 * pieces_of(size) + 1
+    dp = lax.axis_size("dp")
+    shapes = [jax.ShapeDtypeStruct((size, width), jnp.float32)]
+    room = [pltpu.VMEM((size, width), jnp.bfloat16)] * 6
+    room = room + [pltpu.SemaphoreType.DMA((count,)), pltpu.SemaphoreType.DMA((count,))]
+    body, operands = scatter_kernel, (left, right)
+    if grad is not None:
+        body, operands = functools.partial(scatter_exchange_kernel, dp), (left, right, grad)
+        shapes, room = shapes + [side_shape(dp, grad)], room + side_room(dp, grad)
+    elif shard is not None:
+        body, operands = functools.partial(scatter_spread_kernel, dp), (left, right, shard)
+        shapes = shapes + [jax.ShapeDtypeStruct((dp * shard.shape[0], shard.shape[1]), shard.dtype)]
+        room = room + [pltpu.SemaphoreType.DMA((dp - 1,)), pltpu.SemaphoreType.DMA((dp - 1,))]
     return pl.pallas_call(
-        scatter_kernel,
-        in_specs=[vmem(), vmem()],
-        out_specs=vmem(),
-        out_shape=jax.ShapeDtypeStruct((size, width), jnp.float32),
-        scratch_shapes=[pltpu.VMEM((size, width), jnp.bfloat16)] * 6
-        + [pltpu.SemaphoreType.DMA((count,)), pltpu.SemaphoreType.DMA((count,))],
+        body,
+        in_specs=[vmem()] * len(operands),
+        out_specs=[vmem()] * len(shapes),
+        out_shape=shapes,
+        scratch_shapes=room,
         compiler_params=remote_params(ident),
         name=f"scatter_times_{ident}",
-    )(left, right)
+    )(*operands)
 
 
 def opening_kernel(
@@ -404,17 +508,13 @@
     centred = values - jnp.mean(values, axis=-1, keepdims=True)
     factor = lax.rsqrt(jnp.mean(centred * centred, axis=-1, keepdims=True) + 1e-05)
     mine[...] = (centred * factor * placed[0:1, :] + placed[1:2, :]).astype(jnp.bfloat16)
-    landed = []
-
-    def ready(start, rows_count):
-        if not landed:
-            for copy in large:
-                copy.wait_recv()
-            landed.append(True)
-        at = span(start, rows_count)
+    gather_rows(mine, every, sends, recvs, lambda start, rows_count: None)
+    for copy in large:
+        copy.wait_recv()
+    size = mine.shape[0]
+    for block in range(4):
+        at = pl.ds(block * size, size)
         product[at, :] = nn(every[at, :], weights[:, :columns]).astype(jnp.bfloat16)
-
-    gather_rows(mine, every, sends, recvs, ready)
     for copy in little + large:
         copy.wait_send()
 
@@ -539,41 +639,53 @@
         lowered1 = (normalize(inputs)[0] * gains[0] + gains[1]).astype(low)
         all_norm1, projected = gather_times(lowered1, weights[:, :columns], low, 0)
     out_turned = weights[:, columns:]
-    w_fc, w_proj, cotangent_late, lengths, projected = lax.optimization_barrier(
-        (w_fc, w_proj, cotangent, lengths, projected)
-    )
+    w_fc, lengths, projected = lax.optimization_barrier((w_fc, lengths, projected))
     fc_full = lax.all_gather(w_fc, "dp", axis=0, tiled=True)
-    proj_turned = lax.all_gather(w_proj.T, "dp", axis=0, tiled=True)
+    cotangent_late, fc_full = lax.optimization_barrier((cotangent, fc_full))
     grad_all = lax.all_gather(cotangent_late, "tensor", axis=0, tiled=True)
     gain1, gain2, bias2 = gains[0], gains[2], gains[3]
     mixed, sums = attend(projected, lengths, heads)
-    resid = inputs + scatter_times(mixed, out_turned, 1)
+    if small_dp:
+        attended, proj_turned = scatter_times(mixed, out_turned, 1, shard=w_proj.T)
+    else:
+        attended = scatter_times(mixed, out_turned, 1)[0]
+        proj_turned = lax.all_gather(w_proj.T, "dp", axis=0, tiled=True)
+    resid = inputs + attended
     normed2, factor2 = normalize(resid)
     lowered2 = (normed2 * gain2 + bias2).astype(low)
     all_norm2, hidden_pre = gather_times(lowered2, fc_full, jnp.float32, 2)
     hidden, gelu_pull = jax.vjp(gelu_tanh, hidden_pre)
     hidden_low = hidden.astype(low)
-    mlp_rows = lax.psum_scatter(
-        nt(hidden_low, proj_turned).astype(low), "tensor", scatter_dimension=0, tiled=True
-    ).astype(jnp.float32)
-    block_out = (resid + mlp_rows).astype(low)
     hidden_grad = nn(grad_all, proj_turned)
-    proj_grad = inner_rows(grad_all, hidden_low)
+    proj_grad = inner_rows(grad_all, hidden_low).astype(low)
     pre_low = gelu_pull(hidden_grad)[0].astype(low)
-    fc_grad = inner_rows(all_norm2, pre_low)
-    norm2_grad = scatter_times(pre_low, fc_full, 3)
-    proj_sum = scatter_dp(proj_grad).T
-    fc_sum = scatter_dp(fc_grad)
+    fc_grad = inner_rows(all_norm2, pre_low).astype(low)
+    if small_dp:
+        norm2_grad, proj_sum = scatter_times(pre_low, fc_full, 3, grad=proj_grad)
+    else:
+        norm2_grad = scatter_times(pre_low, fc_full, 3)[0]
+        proj_sum, fc_sum = scatter_dp(proj_grad), scatter_dp(fc_grad)
     gain2_part = jnp.sum(norm2_grad * normed2, axis=0)
     bias2_part = jnp.sum(norm2_grad, axis=0)
     resid_grad = cotangent.astype(jnp.float32) + norm_back(norm2_grad, normed2, factor2, gain2)
-    resid_all, mixed_grad = gather_times(resid_grad.astype(low), out_turned, low, 4)
+    if small_dp:
+        resid_all, mixed_grad, fc_sum = gather_times(resid_grad.astype(low), out_turned, low, 4, grad=fc_grad)
+    else:
+        resid_all, mixed_grad = gather_times(resid_grad.astype(low), out_turned, low, 4)
+    hidden_late, mixed_grad = lax.optimization_barrier((hidden_low, mixed_grad))
+    mlp_rows = lax.psum_scatter(
+        nt(hidden_late, proj_turned).astype(low), "tensor", scatter_dimension=0, tiled=True
+    ).astype(jnp.float32)
+    block_out = (resid + mlp_rows).astype(low)
     qkv_grad_low = attend_back(projected, mixed, mixed_grad, sums, lengths, heads)
     last_grad = jnp.concatenate(
         [inner_rows(all_norm1, qkv_grad_low).astype(low), inner_rows(resid_all, mixed).astype(low)], axis=1
     )
-    last_sum = scatter_dp(last_grad)
-    norm1_grad = scatter_times(qkv_grad_low, weights[:, :columns], 5)
+    if small_dp:
+        norm1_grad, last_sum = scatter_times(qkv_grad_low, weights[:, :columns], 5, grad=last_grad)
+    else:
+        norm1_grad = scatter_times(qkv_grad_low, weights[:, :columns], 5)[0]
+        last_sum = scatter_dp(last_grad)
     normed1, factor1 = normalize(inputs)
     input_grad = (resid_grad + norm_back(norm1_grad, normed1, factor1, gain1)).astype(low)
     parts = jnp.stack([jnp.sum(norm1_grad * normed1, axis=0), jnp.sum(norm1_grad, axis=0), gain2_part, bias2_part])
@@ -588,7 +700,7 @@
         last_sum[:, :columns].reshape(depth, 3, local),
         last_sum[:, columns:].T,
         fc_sum,
-        proj_sum,
+        proj_sum.T,
         shares[0],
         shares[1],
         shares[2],

time: 468 us -> 450 us (0.962)
  waiting for transfers between devices: 65.2 us -> 53.3 us
    all_gather x1, waiting for transfers between devices: 0.01 us -> 53.2 us  [on_device(): fc_full = lax.all_gather(w_fc, 'dp', axis=0, tiled=True)]
    reduce_scatter x3 -> x1, waiting for transfers between devices: 34.8 us -> 0.01 us  [on_device(): lax.psum_scatter(nt(hidden_late, proj_turned).astype(low), 'tensor', scat...]
    unnamed x8 -> x3, waiting for transfers between devices: 19.1 us -> 0.05 us
    all_gather x1, waiting for transfers between devices: 11.2 us -> 0.02 us  [on_device(): grad_all = lax.all_gather(cotangent_late, 'tensor', axis=0, tiled=True)]
    unnamed x35 -> x54, local copies, waits for them, and re-layouts: 15.2 us -> 12.6 us
  transfers between devices with their start and end apart: 7 -> 3, of which waited for: 3 -> 1; matrix products, arithmetic and copies ran while one was open for 15% -> 6% of each run, Pallas kernels for 56% -> 42%
where the time goes in v3:
time: 450 us; the launch traced here: 442 us
  Pallas kernels  297 us (66%)
  waiting for transfers between devices  53.3 us (12%)
  matrix products  35.1 us (8%)
  local copies, waits for them, and re-layouts  21.3 us (5%)
  other arithmetic  20.9 us (5%)
  between operations  14.5 us (3%)
    pallas_call x3, Pallas kernels, scatter_times(): pl.pallas_call(body, in_specs=[vmem()] * len(operands), out_specs=[vmem()...  102 us
    pallas_call x2, Pallas kernels, gather_times(): pl.pallas_call(body, in_specs=[vmem()] * len(operands), out_specs=[vmem()...  63.1 us
    all_gather x1, waiting for transfers between devices, on_device(): fc_full = lax.all_gather(w_fc, 'dp', axis=0, tiled=True)  53.2 us
    pallas_call x1, Pallas kernels, attend_back(): pl.pallas_call(functools.partial(backward_kernel, heads), grid=(heads,),...  45.2 us
    pallas_call x1, Pallas kernels, opening(): pl.pallas_call(functools.partial(opening_kernel, columns), in_specs=[vmem...  42.6 us
    pallas_call x1, Pallas kernels, attend(): pl.pallas_call(functools.partial(forward_kernel, heads), grid=(heads,), i...  34.6 us
    dot_general x4, matrix products, inner_rows(): lax.dot_general(left, right, (((0,), (0,)), ((), ())), preferred_element_...  16.2 us
    unnamed x54, local copies, waits for them, and re-layouts  12.6 us
  transfers between devices with their start and end apart: 3, of which 1 were waited for; matrix products, arithmetic and copies ran while one was open for 6% of the time, Pallas kernels for 42%

profile of v3, /device:TPU:0, one launch (start us, length us, event | category | flops | bytes accessed | tf_op | source)
XLA Modules:
  0.0 442.1 jit_solution(14715171324610449475)
XLA Ops:
  7.2 0.0 all-gather.3.cloned.1.call-start
  7.2 0.7 maximum_convert_fusion
  8.0 0.1 tile.10
  8.1 0.9 copy.36
  8.9 0.0 copy-start.5
  9.0 1.1 copy.35
  10.0 0.2 copy.37
  10.2 0.6 concatenate.14.small
  10.8 0.7 pad_maximum_fusion.1.shard
  11.6 42.6 %opening.1 = (bf16[2560,768]{1,0:T(8,128)(2,1)}, bf16[2560,576]{1,0:T(8,128)(2,1)}, bf16[768,768]{1,0:T(8,128)(2,1)}, f32[8,768]{1,0:T(8,128)}) custom-call(bf16[640,768]{1,0:T(8,128)(2,1)} %tokens.1, f32[8,768]{1,0:T(8,128)} %concatenate.14.small, bf16[96,768]{1,0:T(8,128)(2,1)} %pad_maximum_fusion.1.shard), custom_call_target="tpu_custom_call" | custom-call | tf_op jit(solution)/shard_map/opening/pallas_call | solution.py:527
  54.2 0.0 all-gather.3.cloned.1.call-update
  54.2 0.0 all-gather.5.cloned.1.call-start
  54.2 53.2 %all-gather.3.cloned.1.call-done.weight.right = bf16[768,768]{1,0:T(8,128)(2,1)} async-done(((bf16[96,768]{1,0:T(8,128)(2,1)}), bf16[768,768]{1,0:T(8,128)(2,1)}) %all-gather.3.cloned.1.call-update) | async-done | bytes 1179664 | tf_op jit(solution)/shard_map/all_gather | solution.py:643
  107.5 0.0 all-gather.5.cloned.1.call-update
  107.5 0.0 reduce-scatter.2.cloned.1.call-start
  107.5 1.9 slice.38.right.weight
  109.5 1.9 copy-done
  111.4 34.6 %attend.1 = (bf16[2560,192]{1,0:T(8,128)(2,1)S(1)}, f32[3,1,2560]{2,1,0:T(1,128)S(1)}) custom-call(s32[1,8]{1,0:T(1,128)S(1)} %copy-done.5, bf16[2560,576]{1,0:T(8,128)(2,1)S(1)} %copy-done), custom_call_target="tpu_custom_call" | custom-call | tf_op jit(solution)/shard_map/attend/pallas_call | solution.py:133
  146.1 1.1 copy-done.2
  147.2 31.0 %scatter_times_1.1 = (f32[640,768]{1,0:T(8,128)}, bf16[768,768]{1,0:T(8,128)(2,1)}) custom-call(bf16[2560,192]{1,0:T(8,128)(2,1)} %copy-done.2, bf16[768,192]{1,0:T(8,128)(2,1)} %slice.38.right.weight, bf16[96,768]{1,0:T(8,128)(2,1)} %bitcast.37), custom_call_target="tpu_custom_call" | custom-call | tf_op jit(solution)/shard_map/scatter_times_1/pallas_call | solution.py:476
  178.2 0.9 slice_reduce_fusion
  179.1 0.2 convert_reduce_fusion
  179.3 2.2 fusion.24
  181.6 0.4 multiply_reduce_fusion.2
  181.9 1.3 add_convert_fusion.1.mine
  183.3 30.9 %gather_times_2.1 = (bf16[2560,768]{1,0:T(8,128)(2,1)}, f32[2560,768]{1,0:T(8,128)}) custom-call(bf16[640,768]{1,0:T(8,128)(2,1)} %add_convert_fusion.1.mine, bf16[768,768]{1,0:T(8,128)(2,1)} %all-gather.3.cloned.1.call-done.weight.right), custom_call_target="tpu_custom_call" | custom-call | tf_op jit(solution)/shard_map/gather_times_2/pallas_call | solution.py:390
  214.2 0.0 all-gather.5.cloned.1.call-done
  214.2 11.7 %fusion.6 = (bf16[2560,768]{1,0:T(8,128)(2,1)S(1)}, bf16[2560,768]{1,0:T(8,128)(2,1)S(1)}) fusion(f32[2560,768]{1,0:T(8,128)} %get-tuple-element.43, bf16[2560,768]{1,0:T(8,128)(2,1)} %all-gather.5.cloned.1.call-done, bf16[768,768]{1,0:T(8,128)(2,1)} %get-tuple-element.45), kind=kOutput, calls=%fused_computation.8 | convolution fusion | flops 3063152640 | bytes 20840448 | tf_op jit(solution)/shard_map/dot_general | solution.py:22
  226.0 4.5 %convolution_convert_fusion.1.grad = bf16[768,768]{1,0:T(8,128)(2,1)} fusion(bf16[2560,768]{1,0:T(8,128)(2,1)S(1)} %copy-done.21, bf16[2560,768]{1,0:T(8,128)(2,1)S(1)} %get-tuple-element.103.left), kind=kOutput, calls=%fused_computation.35 | convolution fusion | flops 3020488704 | bytes 9043968 | tf_op jit(solution)/shard_map/dot_general | solution.py:605
  230.5 0.5 copy-done.20
  231.0 4.5 %convolution_convert_fusion.2.grad = bf16[768,768]{1,0:T(8,128)(2,1)} fusion(bf16[2560,768]{1,0:T(8,128)(2,1)S(1)} %copy-done.20, bf16[2560,768]{1,0:T(8,128)(2,1)S(1)} %get-tuple-element.49), kind=kOutput, calls=%fused_computation.36 | convolution fusion | flops 3020488704 | bytes 9043968 | tf_op jit(solution)/shard_map/dot_general | solution.py:605
  235.5 34.2 %scatter_times_3.1 = (f32[640,768]{1,0:T(8,128)}, f32[96,768]{1,0:T(8,128)}) custom-call(bf16[2560,768]{1,0:T(8,128)(2,1)} %copy-done.12, bf16[768,768]{1,0:T(8,128)(2,1)} %all-gather.3.cloned.1.call-done.weight.right, bf16[768,768]{1,0:T(8,128)(2,1)} %convolution_convert_fusion.2.grad), custom_call_target="tpu_custom_call" | custom-call | tf_op jit(solution)/shard_map/scatter_times_3/pallas_call | solution.py:476
  269.7 2.6 multiply_reduce_fusion
  272.4 2.5 fusion.23
  274.9 32.2 %gather_times_4.1 = (bf16[2560,768]{1,0:T(8,128)(2,1)}, bf16[2560,192]{1,0:T(8,128)(2,1)}, f32[96,768]{1,0:T(8,128)}) custom-call(bf16[640,768]{1,0:T(8,128)(2,1)} %get-tuple-element.99.mine, bf16[768,192]{1,0:T(8,128)(2,1)} %slice.38.right.weight, bf16[768,768]{1,0:T(8,128)(2,1)} %convolution_convert_fusion.1.grad), custom_call_target="tpu_custom_call" | custom-call | tf_op jit(solution)/shard_map/gather_times_4/pallas_call | solution.py:390
  307.1 7.3 %convolution_convert_fusion = bf16[2560,768]{1,0:T(8,128)(2,1)} fusion(bf16[2560,768]{1,0:T(8,128)(2,1)} %copy-done.23, bf16[768,768]{1,0:T(8,128)(2,1)S(1)} %copy-done.22), kind=kOutput, calls=%fused_computation.10 | convolution fusion | flops 3021864960 | bytes 9043968 | tf_op jit(solution)/shard_map/dot_general | solution.py:18
  314.3 0.0 reduce-scatter.2.cloned.1.call-update
  314.3 1.2 copy-done.14
  315.6 1.0 slice.41.right
  316.6 0.1 stack.37
  316.7 0.1 stack.38
  316.8 1.3 copy-done.3
  318.1 1.3 copy-done.4
  319.4 45.2 %attend_back.1.left = bf16[2560,576]{1,0:T(8,128)(2,1)S(1)} custom-call(s32[1,8]{1,0:T(1,128)S(1)} %copy-done.5, bf16[2560,576]{1,0:T(8,128)(2,1)} %get-tuple-element.36.qkv_ref, bf16[2560,192]{1,0:T(8,128)(2,1)S(1)} %copy-done.3, bf16[2560,192]{1,0:T(8,128)(2,1)S(1)} %copy-done.4, f32[3,1,2560]{2,1,0:T(1,128)S(1)} %get-tuple-element.51.lse_ref), custom_call_target="tpu_custom_call" | custom-call | tf_op jit(solution)/shard_map/attend_back/pallas_call | solution.py:221
  364.6 3.6 convolution_convert_fusion.3
  368.2 2.2 copy.38
  370.5 3.6 convolution_convert_fusion.4
  374.0 0.2 copy.39
  374.2 1.2 pad_maximum_fusion.grad
  375.4 36.4 %scatter_times_5.1 = (f32[640,768]{1,0:T(8,128)}, f32[96,768]{1,0:T(8,128)}) custom-call(bf16[2560,576]{1,0:T(8,128)(2,1)} %copy-done.1, bf16[768,576]{1,0:T(8,128)(2,1)} %slice.41.right, bf16[768,768]{1,0:T(8,128)(2,1)} %pad_maximum_fusion.grad), custom_call_target="tpu_custom_call" | custom-call | tf_op jit(solution)/shard_map/scatter_times_5/pallas_call | solution.py:476
  411.8 2.5 fusion.17
  414.4 0.1 stack.35
  414.4 0.1 stack.36
  414.5 0.6 pad.5.parts
  415.2 9.7 %sum_vectors.1 = f32[8,128]{1,0:T(8,128)} custom-call(f32[8,8,128]{2,1,0:T(8,128)} %pad.5.parts), custom_call_target="tpu_custom_call" | custom-call | tf_op jit(solution)/shard_map/sum_vectors/pallas_call | solution.py:571
  425.0 0.1 slice_bitcast_fusion
  425.0 0.7 copy.42
  425.8 0.1 copy.40
  425.9 0.9 copy.41
  426.8 0.5 slice_bitcast_fusion.1
  427.4 3.9 fusion.16
  431.3 2.4 add_convert_fusion
  433.7 0.7 copy.45
  434.5 0.7 copy.46
  (54 shorter events, 0.2 us)
Async XLA Ops:
  7.2 100.3 %all-gather.3.cloned.1.call-start = ((), (), s32[]{:S(2)}) async-start(), calls=%async_computation.1 | async-start | bytes 1327104 | tf_op jit(solution)/shard_map/all_gather | solution.py:643
  8.9 100.5 %copy-start.5 = (s32[1,8]{1,0:T(1,128)S(1)}, s32[1,8]{1,0:T(1,128)}, u32[]{:S(2)}) copy-start(s32[1,8]{1,0:T(1,128)} %lengths_ref.1) | copy-start | bytes 100
  54.2 160.0 %all-gather.5.cloned.1.call-start = ((), (), s32[]{:S(2)}) async-start(), calls=%async_computation.2 | async-start | bytes 4915200 | tf_op jit(solution)/shard_map/all_gather | solution.py:645
  107.5 323.8 %reduce-scatter.2.cloned.1.call-start = ((), (), s32[]{:S(2)}) async-start(), calls=%async_computation.3 | async-start | bytes 4915200 | tf_op jit(solution)/shard_map/reduce_scatter | solution.py:676
  109.5 1.9 copy-start
  111.4 67.7 %copy-start.8 = (bf16[640,768]{1,0:T(8,128)(2,1)S(1)}, bf16[640,768]{1,0:T(8,128)(2,1)}, u32[]{:S(2)}) copy-start(bf16[640,768]{1,0:T(8,128)(2,1)} %tokens.1) | copy-start | bytes 2949124
  146.1 1.1 copy-start.2
  181.6 90.8 %copy-start.6 = (f32[640,768]{1,0:T(8,128)}, f32[640,768]{1,0:T(8,128)S(1)}, u32[]{:S(2)}) copy-start(f32[640,768]{1,0:T(8,128)S(1)} %get-tuple-element.102) | copy-start | bytes 5898244
  214.2 11.7 %copy-start.21 = (bf16[2560,768]{1,0:T(8,128)(2,1)S(1)}, bf16[2560,768]{1,0:T(8,128)(2,1)}, u32[]{:S(2)}) copy-start(bf16[2560,768]{1,0:T(8,128)(2,1)} %get-tuple-element.47) | copy-start | bytes 11796484
  225.9 4.6 %copy-start.12 = (bf16[2560,768]{1,0:T(8,128)(2,1)}, bf16[2560,768]{1,0:T(8,128)(2,1)S(1)}, u32[]{:S(2)}) copy-start(bf16[2560,768]{1,0:T(8,128)(2,1)S(1)} %get-tuple-element.103.left) | copy-start | bytes 11796484
  225.9 4.6 %copy-start.23 = (bf16[2560,768]{1,0:T(8,128)(2,1)}, bf16[2560,768]{1,0:T(8,128)(2,1)S(1)}, u32[]{:S(2)}) copy-start(bf16[2560,768]{1,0:T(8,128)(2,1)S(1)} %get-tuple-element.49) | copy-start | bytes 11796484
  225.9 5.1 %copy-start.20 = (bf16[2560,768]{1,0:T(8,128)(2,1)S(1)}, bf16[2560,768]{1,0:T(8,128)(2,1)}, u32[]{:S(2)}) copy-start(bf16[2560,768]{1,0:T(8,128)(2,1)} %all-gather.5.cloned.1.call-done) | copy-start | bytes 11796484
  269.7 2.7 copy-start.10
  269.7 2.7 copy-start.13
  274.9 32.2 %copy-start.22 = (bf16[768,768]{1,0:T(8,128)(2,1)S(1)}, bf16[768,768]{1,0:T(8,128)(2,1)}, u32[]{:S(2)}) copy-start(bf16[768,768]{1,0:T(8,128)(2,1)} %get-tuple-element.45) | copy-start | bytes 3538948
  314.3 1.3 copy-start.14
  316.8 1.3 copy-start.3
  318.1 1.3 copy-start.4
  319.4 45.2 %copy-start.19 = (bf16[2560,768]{1,0:T(8,128)(2,1)S(1)}, bf16[2560,768]{1,0:T(8,128)(2,1)}, u32[]{:S(2)}) copy-start(bf16[2560,768]{1,0:T(8,128)(2,1)} %get-tuple-element.52) | copy-start | bytes 11796484
  364.6 3.6 copy-start.1
  370.5 3.7 copy-start.11
  375.4 36.4 %copy-start.9 = (bf16[640,768]{1,0:T(8,128)(2,1)S(1)}, bf16[640,768]{1,0:T(8,128)(2,1)}, u32[]{:S(2)}) copy-start(bf16[640,768]{1,0:T(8,128)(2,1)} %tokens.1) | copy-start | bytes 2949124
  411.8 13.1 %copy-start.15 = (f32[96,768]{1,0:T(8,128)S(1)}, f32[96,768]{1,0:T(8,128)}, u32[]{:S(2)}) copy-start(f32[96,768]{1,0:T(8,128)} %get-tuple-element.55) | copy-start | bytes 884740
  424.9 1.9 copy-start.18
  427.4 3.9 copy-start.7
  431.3 2.5 copy-start.17
  431.3 3.2 copy-start.16
Sparse Core Ops, SparseCore 0:
  54.3 53.1 all-gather.2
  109.0 31.6 all-gather.4
  314.5 45.0 reduce-scatter.1
